TPU v7x, 32 devices: a whole 2x2x4 slice. The times are simulated.
32 devices in a mesh: lat: 16 (over z, y, core), lon: 2 (over x).
Axes of the slice: x: 2, y: 2, z: 4, core: 2. Of those that a mesh axis runs over, the one named last changes fastest.
Arguments:
- eastward_speed_face: float32 [72, 512, 256], P(None, 'lat', 'lon'), may hold values from -6 to 6
- northward_speed_face: float32 [72, 512, 256], P(None, 'lat', 'lon'), may hold values from -6 to 6
- stratum_extent_east_face: float32 [72, 512, 256], P(None, 'lat', 'lon'), may hold values from 0.5 to 2
- stratum_extent_north_face: float32 [72, 512, 256], P(None, 'lat', 'lon'), may hold values from 0.5 to 2
- northward_span_east_face: float32 [512, 256], P('lat', 'lon'), may hold values from 0.5 to 2
- eastward_span_north_face: float32 [512, 256], P('lat', 'lon'), may hold values from 0.5 to 2
- ocean_flag_east_face: int32 [72, 512, 256], P(None, 'lat', 'lon'), may hold values 0 or 1
- ocean_flag_north_face: int32 [72, 512, 256], P(None, 'lat', 'lon'), may hold values 0 or 1
- counterpart_across_seam: int32 [256], replicated, may hold values from 0 to 255, as said below
Outputs:
- eastward_speed_next: float32 [72, 512, 256], P(None, 'lat', 'lon')
- northward_speed_next: float32 [72, 512, 256], P(None, 'lat', 'lon')
Inputs may be any that keep to these rules, and one draw needn't show every extreme that they name: counterpart_across_seam[i] = (p - 1 - i) mod 256 for one pivot p drawn anew in each draw; it is its own inverse.
All inputs are finite; a program needn't handle non-finite values. No bound on the sum of `ocean_flag_east_face` or of `ocean_flag_north_face` on one device may be relied on, other than what follows from the above.
Results may differ from a plain program's by a relative error of at most 0.00002.
Values sent between devices are 32-bit elements; how exact they have to be, the bound alone decides.
A program may use at most 128 MiB of HBM per device.

v0:
```python
import functools

import jax
import jax.numpy as jnp
from jax import lax
from jax.experimental import pallas as pl
from jax.experimental.pallas import tpu as pltpu
from jax.sharding import PartitionSpec as P

time_step = 0.2
lanes = 128
group = 8
spare = 8
MESH = pl.DeviceIdType.MESH


def chunk_count(levels):
    groups = levels // group
    return next(c for c in (3, 2, 1) if groups % c == 0)


def roll(x, shift):
    return pltpu.roll(x, shift % lanes, 1)


def exchange_kernel(
    nlat, nlon, levels, rows,
    u_hbm, v_hbm, eu_hbm, ev_hbm, su_hbm, sv_hbm, mu_hbm, mv_hbm,
    um_x, vm_x, tu_x, tv_x, cu_x, cv_x, packs, corner_u, corner_v, band,
    u_in, v_in, eu_in, ev_in, su_in, sv_in, mu_in, mv_in,
    pack_own, corner_u_own, corner_v_own,
    load_sem, span_sem, up_send, up_recv, down_send, down_recv,
    lon_send, lon_recv, diag_send, diag_recv, band_send, band_recv,
):
    chunks = chunk_count(levels)
    depth = levels // chunks
    lat = lax.axis_index("lat")
    lon = lax.axis_index("lon")
    right = lax.rem(lon + 1, nlon)
    left = lax.rem(lon + nlon - 1, nlon)
    has_up = lat < nlat - 1
    has_down = lat > 0
    sides = 1 if nlon == 2 else 2

    pairs = (
        (u_hbm, u_in), (mu_hbm, mu_in), (eu_hbm, eu_in),
        (v_hbm, v_in), (mv_hbm, mv_in), (ev_hbm, ev_in),
    )
    spans = [
        pltpu.make_async_copy(su_hbm, su_in, span_sem.at[0]),
        pltpu.make_async_copy(sv_hbm, sv_in, span_sem.at[1]),
    ]
    loads = [
        [
            pltpu.make_async_copy(
                a.at[pl.ds(c * depth, depth)], b.at[pl.ds(c * depth, depth), pl.ds(0, rows)], load_sem.at[c, k]
            )
            for k, (a, b) in enumerate(pairs)
        ]
        for c in range(chunks)
    ]
    for copy in spans:
        copy.start()
    for per_chunk in loads:
        for copy in per_chunk:
            copy.start()

    barrier = pltpu.get_barrier_semaphore()

    def greet(where):
        pl.semaphore_signal(barrier, inc=1, device_id=where, device_id_type=MESH)

    greet((lat, right))
    if nlon > 2:
        greet((lat, left))

    @pl.when(has_up)
    def _():
        greet((lat + 1, lon))
        greet((lat + 1, left))

    @pl.when(has_down)
    def _():
        greet((lat - 1, lon))
        greet((lat - 1, right))

    if nlon > 3:
        @pl.when(lat == nlat - 1)
        def _():
            for d in range(2, nlon - 1):
                greet((lat, lax.rem(lon + d, nlon)))

    def arrive():
        @pl.when(lat == 0)
        def _():
            pl.semaphore_wait(barrier, sides + 2)

        @pl.when(has_up & has_down)
        def _():
            pl.semaphore_wait(barrier, sides + 4)

        @pl.when(lat == nlat - 1)
        def _():
            pl.semaphore_wait(barrier, sides + 2 + max(nlon - 3, 0))

    def remote(src, dst, send, recv, where):
        return pltpu.make_async_remote_copy(
            src_ref=src, dst_ref=dst, send_sem=send, recv_sem=recv,
            device_id=where, device_id_type=MESH,
        )

    def up_copies(c):
        part = pl.ds(c * depth, depth)
        where = (lat + 1, lon)
        moves = (
            (um_x.at[pl.ds(rows, 2), part], um_x.at[pl.ds(0, 2), part]),
            (vm_x.at[pl.ds(rows, 2), part], vm_x.at[pl.ds(0, 2), part]),
            (tv_x.at[pl.ds(rows, 1), part], tv_x.at[pl.ds(0, 1), part]),
        )
        return [
            remote(a, b, up_send.at[c, k], up_recv.at[c, k], where)
            for k, (a, b) in enumerate(moves)
        ]

    def down_copies(c):
        part = pl.ds(c * depth, depth)
        where = (lat - 1, lon)
        moves = (
            (um_x.at[pl.ds(2, 2), part], um_x.at[pl.ds(rows + 2, 2), part]),
            (vm_x.at[pl.ds(2, 2), part], vm_x.at[pl.ds(rows + 2, 2), part]),
            (tu_x.at[pl.ds(0, 1), part], tu_x.at[pl.ds(rows, 1), part]),
            (tv_x.at[pl.ds(1, 1), part], tv_x.at[pl.ds(rows + 1, 1), part]),
        )
        return [
            remote(a, b, down_send.at[c, k], down_recv.at[c, k], where)
            for k, (a, b) in enumerate(moves)
        ]

    def lon_copies(c):
        part = pl.ds(c * depth, depth)
        targets = (right,) if nlon == 2 else (right, left)
        return [
            remote(
                pack_own.at[:, part], packs.at[k, :, part],
                lon_send.at[c, k], lon_recv.at[c, k], (lat, target),
            )
            for k, target in enumerate(targets)
        ]

    def corner_down():
        return remote(
            corner_u_own, corner_u, diag_send.at[0], diag_recv.at[0], (lat - 1, right)
        )

    def corner_up():
        return remote(
            corner_v_own, corner_v, diag_send.at[1], diag_recv.at[1], (lat + 1, left)
        )

    def band_copy(c, d):
        part = pl.ds(c * depth, depth)
        return remote(
            band.at[lon, :, part], band.at[lon, :, part],
            band_send.at[c, d], band_recv.at[c, d], (lat, lax.rem(lon + d, nlon)),
        )

    def band_arrival(c, d):
        part = pl.ds(c * depth, depth)
        origin = lax.rem(lon + nlon - d, nlon)
        return remote(
            band.at[lon, :, part], band.at[origin, :, part],
            band_send.at[c, d], band_recv.at[c, d], (lat, lax.rem(lon + d, nlon)),
        )

    lane = lax.broadcasted_iota(jnp.int32, (group, lanes), 1)
    quad = lane // 4
    place = lane % 4
    pitch = rows + spare
    views = [ref.reshape(levels * pitch, lanes) for _, ref in pairs]

    def compute(g, corners):
        cu_corner, cv_corner = corners
        base = g * group
        part = pl.ds(pl.multiple_of(base, group), group)
        zero = jnp.zeros((group, lanes), jnp.float32)
        pack_u, pack_v, pack_t = zero, zero, zero
        for r in range(rows):
            u, mu, eu, v, mv, ev = [
                view[pl.ds(base * pitch + r, group, stride=pitch), :] for view in views
            ]
            mu = mu.astype(jnp.float32)
            mv = mv.astype(jnp.float32)
            um = mu * u
            vm = mv * v
            vol_u = su_in[pl.ds(r, 1), :] * eu
            vol_v = sv_in[pl.ds(r, 1), :] * ev
            tu = vol_u * um
            tv = vol_v * vm
            um_x[r + 2, part, :] = um
            vm_x[r + 2, part, :] = vm
            tu_x[r, part, :] = tu
            tv_x[r + 1, part, :] = tv
            cu_x[r, part, :] = mu * (-time_step / 24.0) / vol_u
            cv_x[r, part, :] = mv * (-time_step / 24.0) / vol_v
            here = quad == r
            pack_u = jnp.where(here, roll(um, 2 + 4 * r), pack_u)
            pack_v = jnp.where(here, roll(vm, 2 + 4 * r), pack_v)
            both = jnp.where(place < 2, roll(tu, 1 + 4 * r), roll(tv, 3 + 4 * r))
            pack_t = jnp.where(here, both, pack_t)
            if r == 0:
                cu_corner = jnp.where(lane == g, pltpu.roll(tu, g + 1, 1), cu_corner)
            if r == rows - 1:
                cv_corner = jnp.where(lane == g, pltpu.roll(tv, g, 1), cv_corner)
                band[lon, 4, part, :] = tu
                band[lon, 5, part, :] = tv
            if r >= rows - 2:
                band[lon, r - rows + 2, part, :] = um
                band[lon, r - rows + 4, part, :] = vm
        pack_own[0, part, :] = pack_u
        pack_own[1, part, :] = pack_v
        pack_own[2, part, :] = pack_t
        return cu_corner, cv_corner

    @pl.when(lat == 0)
    def _():
        um_x[pl.ds(0, 2)] = jnp.zeros((2, levels, lanes), jnp.float32)
        vm_x[pl.ds(0, 2)] = jnp.zeros((2, levels, lanes), jnp.float32)
        tv_x[pl.ds(0, 1)] = jnp.zeros((1, levels, lanes), jnp.float32)
        corner_v[...] = jnp.zeros((group, lanes), jnp.float32)

    for copy in spans:
        copy.wait()
    corners = (jnp.zeros((group, lanes), jnp.float32),) * 2
    for c in range(chunks):
        for copy in loads[c]:
            copy.wait()
        per = depth // group
        corners = lax.fori_loop(c * per, (c + 1) * per, compute, corners)
        if c == 0:
            arrive()

        for copy in lon_copies(c):
            copy.start()

        @pl.when(has_down)
        def _():
            for copy in down_copies(c):
                copy.start()

        @pl.when(has_up)
        def _():
            for copy in up_copies(c):
                copy.start()

        @pl.when(lat == nlat - 1)
        def _():
            for d in range(1, nlon):
                band_copy(c, d).start()

    corner_u_own[...], corner_v_own[...] = corners

    @pl.when(has_down)
    def _():
        corner_down().start()

    @pl.when(has_up)
    def _():
        corner_up().start()

    for c in range(chunks):
        for copy in lon_copies(c):
            copy.wait()

        @pl.when(has_down)
        def _():
            for copy in down_copies(c):
                copy.wait_send()
            for copy in up_copies(c):
                copy.wait_recv()

        @pl.when(has_up)
        def _():
            for copy in up_copies(c):
                copy.wait_send()
            for copy in down_copies(c):
                copy.wait_recv()

        @pl.when(lat == nlat - 1)
        def _():
            for d in range(1, nlon):
                band_copy(c, d).wait_send()
                band_arrival(c, d).wait_recv()

    @pl.when(has_down)
    def _():
        corner_down().wait_send()
        corner_up().wait_recv()

    @pl.when(has_up)
    def _():
        corner_up().wait_send()
        corner_down().wait_recv()


def stencil_kernel(
    nlat, nlon, levels, rows,
    fold_ref, um_x, vm_x, tu_x, tv_x, cu_x, cv_x, packs, corner_u, corner_v, band,
    u_out, v_out,
    high, high_left, beside, moved, u_buf, v_buf, out_sem,
):
    lat = lax.axis_index("lat")
    lon = lax.axis_index("lon")
    groups = levels // group
    width = nlon * lanes
    lane = lax.broadcasted_iota(jnp.int32, (group, lanes), 1)
    top = lat == nlat - 1

    @pl.when(top)
    def _():
        first = fold_ref[0]
        own = lax.rem(first - lon * lanes - lane + 2 * width, width)
        before = jnp.zeros_like(lane) + lax.rem(first - lon * lanes + 1 + 2 * width, width)

        def pick(k, part, index):
            block = index // lanes
            spot = index % lanes
            got = jnp.zeros((group, lanes), jnp.float32)
            for b in range(nlon):
                taken = jnp.take_along_axis(
                    band[b, k, part, :], spot, axis=1, mode="promise_in_bounds"
                )
                got = jnp.where(block == b, taken, got)
            return -got

        def fill(g, carry):
            part = pl.ds(pl.multiple_of(g * group, group), group)
            high[0, part, :] = pick(1, part, own)
            high[1, part, :] = pick(0, part, own)
            high[2, part, :] = pick(3, part, own)
            high[3, part, :] = pick(2, part, own)
            high[4, part, :] = pick(4, part, own)
            high[5, part, :] = pick(5, part, own)
            high_left[part, :] = pick(4, part, before)
            return carry

        lax.fori_loop(0, groups, fill, 0)

    @pl.when(lat < nlat - 1)
    def _():
        def fill(g, carry):
            part = pl.ds(pl.multiple_of(g * group, group), group)
            high[0, part, :] = um_x[rows + 2, part, :]
            high[1, part, :] = um_x[rows + 3, part, :]
            high[2, part, :] = vm_x[rows + 2, part, :]
            high[3, part, :] = vm_x[rows + 3, part, :]
            high[4, part, :] = tu_x[rows, part, :]
            high[5, part, :] = tv_x[rows + 1, part, :]
            high_left[part, :] = pltpu.roll(corner_u[...], lanes - 1 - g, 1)
            return carry

        lax.fori_loop(0, groups, fill, 0)

    place = lane % 4
    pitch = rows + spare
    u_view = u_buf.reshape(levels * pitch, lanes)
    v_view = v_buf.reshape(levels * pitch, lanes)

    def q(a, b, c, d):
        return 7.0 * (b + c) - (a + d)

    def out_copies(g):
        part = pl.ds(g * group, group)
        return (
            pltpu.make_async_copy(u_buf.at[part, pl.ds(0, rows)], u_out.at[part], out_sem.at[g, 0]),
            pltpu.make_async_copy(v_buf.at[part, pl.ds(0, rows)], v_out.at[part], out_sem.at[g, 1]),
        )

    def readers(part):
        def um(j):
            return um_x[j + 2, part, :] if j < rows else high[j - rows, part, :]

        def vm(j):
            return vm_x[j + 2, part, :] if j < rows else high[j - rows + 2, part, :]

        def tu(j):
            return tu_x[j, part, :] if j < rows else high[4, part, :]

        def tv(j):
            return tv_x[j + 1, part, :] if j < rows else high[5, part, :]

        return um, vm, tu, tv

    def unpack(g, carry):
        part = pl.ds(pl.multiple_of(g * group, group), group)
        if packs.shape[0] == 1:
            pack_u, pack_v, pack_t = [packs[0, k, part, :] for k in range(3)]
        else:
            pack_u, pack_v = [
                jnp.where(place < 2, packs[0, k, part, :], packs[1, k, part, :])
                for k in range(2)
            ]
            pack_t = jnp.where(place < 1, packs[0, 2, part, :], packs[1, 2, part, :])
        for j in range(rows):
            beside[0, j, part, :] = roll(pack_u, -(4 * j + 2))
            beside[1, j, part, :] = roll(pack_v, -(4 * j + 2))
            beside[2, j, part, :] = roll(pack_t, -(4 * j + 1))
            beside[3, j, part, :] = roll(pack_t, -(4 * j + 3))
        return carry

    lax.fori_loop(0, groups, unpack, 0)

    def shift(g, carry):
        part = pl.ds(pl.multiple_of(g * group, group), group)
        um, vm, tu, tv = readers(part)
        tv_low = jnp.where(
            lane == 0, pltpu.roll(corner_v[...], lax.rem(lanes - g, lanes), 1), tv(-1)
        )
        moved[11, 0, part, :] = roll(tv_low, -1)
        moved[11, 1, part, :] = roll(
            jnp.where(lane == lanes - 1, high_left[part, :], tu(rows)), 1
        )
        for j in range(rows):
            for k, own in ((0, um(j)), (4, vm(j))):
                halo = beside[k // 4, j, part, :]
                low = jnp.where(lane >= lanes - 2, halo, own)
                upper = jnp.where(lane < 2, halo, own)
                moved[k, j, part, :] = roll(low, 2)
                moved[k + 1, j, part, :] = roll(jnp.where(lane == lanes - 1, halo, own), 1)
                moved[k + 2, j, part, :] = roll(jnp.where(lane == 0, halo, own), -1)
                moved[k + 3, j, part, :] = roll(upper, -2)
            own, halo = tu(j), beside[2, j, part, :]
            moved[8, j, part, :] = roll(jnp.where(lane == lanes - 1, halo, own), 1)
            moved[9, j, part, :] = roll(jnp.where(lane == 0, halo, own), -1)
            moved[10, j, part, :] = roll(jnp.where(lane == 0, beside[3, j, part, :], tv(j)), -1)
        return carry

    lax.fori_loop(0, groups, shift, 0)

    def step(g, carry):
        part = pl.ds(pl.multiple_of(g * group, group), group)
        um, vm, tu, tv = readers(part)

        def tu_sides(j):
            if j < rows:
                return tu(j), moved[8, j, part, :], moved[9, j, part, :]
            return tu(j), moved[11, 1, part, :], None

        def around(k, j, own):
            w2, w1, e1, e2 = [moved[k + i, j, part, :] for i in range(4)]
            return q(w2, w1, own, e1), q(w1, own, e1, e2)

        def fvf(j):
            east = moved[11, 0, part, :] if j < 0 else moved[10, j, part, :]
            return (tv(j) + east) * q(um(j - 1), um(j), um(j + 1), um(j + 2))

        def fvt(j):
            return (tv(j - 1) + tv(j)) * q(vm(j - 2), vm(j - 1), vm(j), vm(j + 1))

        fvf_low = fvf(-1)
        fvt_low = fvt(0)
        tu_own, tu_west, tu_east = tu_sides(0)
        for j in range(rows):
            fvf_high = fvf(j)
            fvt_high = fvt(j + 1)
            um_own = um(j)
            vm_own = vm(j)
            q_west, q_east = around(0, j, um_own)
            du = (tu_own + tu_east) * q_east - (tu_west + tu_own) * q_west
            du = du + (fvf_high - fvf_low)
            next_own, next_west, next_east = tu_sides(j + 1)
            q_west, q_east = around(4, j, vm_own)
            dv = (tu_own + next_own) * q_east - (tu_west + next_west) * q_west
            dv = dv + (fvt_high - fvt_low)
            where = pl.ds(g * (group * pitch) + j, group, stride=pitch)
            u_view[where, :] = um_own + cu_x[j, part, :] * du
            v_view[where, :] = vm_own + cv_x[j, part, :] * dv
            fvf_low, fvt_low = fvf_high, fvt_high
            tu_own, tu_west, tu_east = next_own, next_west, next_east
        for copy in out_copies(g):
            copy.start()
        return carry

    lax.fori_loop(0, groups, step, 0)

    def finish(g, carry):
        for copy in out_copies(g):
            copy.wait()
        return carry

    lax.fori_loop(0, groups, finish, 0)


def local(nlat, nlon, u, v, eu, ev, su, sv, mu, mv, fold):
    u, v, eu, ev, su, sv, mu, mv = [
        pltpu.with_memory_space_constraint(x, pltpu.HBM) for x in (u, v, eu, ev, su, sv, mu, mv)
    ]
    levels, rows, _ = u.shape
    chunks = chunk_count(levels)
    sides = 1 if nlon == 2 else 2
    f32 = jnp.float32
    vmem = pl.BlockSpec(memory_space=pltpu.VMEM)
    hbm = pl.BlockSpec(memory_space=pltpu.HBM)
    shapes = [
        (rows + 4, levels, lanes),
        (rows + 4, levels, lanes),
        (rows + 1, levels, lanes),
        (rows + 2, levels, lanes),
        (rows, levels, lanes),
        (rows, levels, lanes),
        (sides, 3, levels, lanes),
        (group, lanes),
        (group, lanes),
        (nlon, 6, levels, lanes),
    ]
    block = (levels, rows, lanes)
    roomy = (levels, rows + spare, lanes)
    dma = pltpu.SemaphoreType.DMA
    fields = pl.pallas_call(
        functools.partial(exchange_kernel, nlat, nlon, levels, rows),
        out_shape=[pltpu.VMEM(s, f32) for s in shapes],
        in_specs=[hbm] * 8,
        out_specs=[vmem] * len(shapes),
        scratch_shapes=[
            pltpu.VMEM(roomy, f32),
            pltpu.VMEM(roomy, f32),
            pltpu.VMEM(roomy, f32),
            pltpu.VMEM(roomy, f32),
            pltpu.VMEM((rows, lanes), f32),
            pltpu.VMEM((rows, lanes), f32),
            pltpu.VMEM(roomy, jnp.int32),
            pltpu.VMEM(roomy, jnp.int32),
            pltpu.VMEM((3, levels, lanes), f32),
            pltpu.VMEM((group, lanes), f32),
            pltpu.VMEM((group, lanes), f32),
            dma((chunks, 6)),
            dma((2,)),
            dma((chunks, 3)),
            dma((chunks, 3)),
            dma((chunks, 4)),
            dma((chunks, 4)),
            dma((chunks, sides)),
            dma((chunks, sides)),
            dma((2,)),
            dma((2,)),
            dma((chunks, nlon)),
            dma((chunks, nlon)),
        ],
        compiler_params=pltpu.CompilerParams(
            collective_id=0, has_side_effects=True, vmem_limit_bytes=16 * 1024 * 1024
        ),
        name="exchange",
    )(u, v, eu, ev, su, sv, mu, mv)
    result = pl.pallas_call(
        functools.partial(stencil_kernel, nlat, nlon, levels, rows),
        out_shape=[jax.ShapeDtypeStruct(block, f32)] * 2,
        in_specs=[pl.BlockSpec(memory_space=pltpu.SMEM)] + [vmem] * len(shapes),
        out_specs=[hbm] * 2,
        scratch_shapes=[
            pltpu.VMEM((6, levels, lanes), f32),
            pltpu.VMEM((levels, lanes), f32),
            pltpu.VMEM((4, rows, levels, lanes), f32),
            pltpu.VMEM((12, rows, levels, lanes), f32),
            pltpu.VMEM(roomy, f32),
            pltpu.VMEM(roomy, f32),
            dma((levels // group, 2)),
        ],
        compiler_params=pltpu.CompilerParams(vmem_limit_bytes=32 * 1024 * 1024),
        name="stencil",
    )(fold, *fields)
    return tuple(result)


def solution(mesh):
    level_rows_columns = P(None, "lat", "lon")
    return jax.shard_map(
        functools.partial(local, mesh.shape["lat"], mesh.shape["lon"]),
        mesh=mesh,
        in_specs=(
            level_rows_columns,
            level_rows_columns,
            level_rows_columns,
            level_rows_columns,
            P("lat", "lon"),
            P("lat", "lon"),
            level_rows_columns,
            level_rows_columns,
            P(),
        ),
        out_specs=(level_rows_columns,) * 2,
        check_vma=False,
    )
```

profile of v0, /device:TPU:29, one launch (start us, length us, event | category | flops | bytes accessed | tf_op | source)
XLA Modules:
  0.0 22.2 jit_solution(5318723377971563219)
XLA Ops:
  0.6 0.0 copy-start
  0.6 11.2 %exchange.1 = (f32[36,72,128]{2,1,0:T(8,128)S(1)}, f32[36,72,128]{2,1,0:T(8,128)S(1)}, f32[33,72,128]{2,1,0:T(8,128)S(1)}, f32[34,72,128]{2,1,0:T(8,128)S(1)}, f...) custom-call(f32[72,32,128]{2,1,0:T(8,128)} %u_hbm.1, ...), custom_call_target="tpu_custom_call" | custom-call | tf_op jit(solution)/shard_map/exchange/pallas_call | solution.py:518
  11.9 0.0 copy-done
  11.9 10.3 %stencil.1 = (f32[72,32,128]{2,1,0:T(8,128)}, f32[72,32,128]{2,1,0:T(8,128)}) custom-call(s32[256]{0:T(256)S(1)} %copy-done, f32[36,72,128]{2,1,0:T(8,128)S(1)} %get-tuple-element.12.um_x, f32[36,72,128]{2,1,0:T(8,128)S(1)} %get-tuple-element.13.vm_x, f32[33,72,128]{2,1,0:T(8,128)S(1)} %get-tuple-element.14.tu_x, f32[34,72,128]{2,1,0:T(8,128)S(1)} %get-tuple-element.15.tv_x, ...), custom_call_target="tpu_custom_call" | custom-call | tf_op jit(solution)/shard_map/stencil/pallas_call | solution.py:553
Async XLA Ops:
  0.6 11.3 %copy-start = (s32[256]{0:T(256)S(1)}, s32[256]{0:T(256)}, u32[]{:S(2)}) copy-start(s32[256]{0:T(256)} %fold_ref.1) | copy-start | bytes 3076
where the time goes:
time: 22.4 us; the launch traced here: 22.2 us
  Pallas kernels  21.6 us (96%)
  between operations  0.66 us (3%)
    pallas_call x1, Pallas kernels, local(): pl.pallas_call(functools.partial(exchange_kernel, nlat, nlon, levels, row...  11.2 us
    pallas_call x1, Pallas kernels, local(): pl.pallas_call(functools.partial(stencil_kernel, nlat, nlon, levels, rows...  10.3 us

commit v1 on v0

v1 whole, which is shorter than its diff:
```python
import functools

import jax
import jax.numpy as jnp
from jax import lax
from jax.experimental import pallas as pl
from jax.experimental.pallas import tpu as pltpu
from jax.sharding import PartitionSpec as P

time_step = 0.2
scale = -time_step / 24.0
lanes = 128
group = 8
pad = 8
MESH = pl.DeviceIdType.MESH
f32 = jnp.float32


def chunk_count(levels, per):
    count = levels // per
    return next(c for c in (3, 2, 1) if count % c == 0)


def roll(x, shift):
    return pltpu.roll(x, shift % lanes, 1)


def vroll(x, shift):
    return pltpu.roll(x, shift % group, 0)


def q(a, b, c, d):
    return 7.0 * (b + c) - (a + d)


def exchange_kernel(
    nlat, nlon, levels, rows,
    u_hbm, v_hbm, eu_hbm, ev_hbm, su_hbm, sv_hbm, mu_hbm, mv_hbm,
    u_part, v_part, low_own, high_own, keep, side, up_in, down_in, corner_u, corner_v, band,
    u_in, v_in, eu_in, ev_in, su_in, sv_in, mu_in, mv_in,
    edge_f, edge_m, um_n, vm_n, tv_n, cu_n, cv_n, um_t, vm_t, tu_t, ts_t,
    pack_own, pack_in, edge_own, edge_in, corner_u_own, corner_v_own, fix,
    edge_sem, load_sem, span_sem, up_send, up_recv, down_send, down_recv,
    lon_send, lon_recv, side_send, side_recv, diag_send, diag_recv, band_send, band_recv,
):
    per = lanes // rows
    tall = rows // group
    blocks = levels // per
    chunks = chunk_count(levels, per)
    depth = levels // chunks
    blocks_in = blocks // chunks
    groups = levels // group
    pitch = rows + pad
    lat = lax.axis_index("lat")
    lon = lax.axis_index("lon")
    right = lax.rem(lon + 1, nlon)
    left = lax.rem(lon + nlon - 1, nlon)
    has_up = lat < nlat - 1
    has_down = lat > 0
    sides = 1 if nlon == 2 else 2
    picked = (0, 1, rows - 2, rows - 1)

    edges = [
        pltpu.make_async_copy(a.at[:, r, :], b.at[k, e], edge_sem.at[4 * s + e])
        for s, (a, b, k) in enumerate((
            (u_hbm, edge_f, 0), (mu_hbm, edge_m, 0), (v_hbm, edge_f, 1),
            (mv_hbm, edge_m, 1), (eu_hbm, edge_f, 2), (ev_hbm, edge_f, 3),
        ))
        for e, r in enumerate(picked)
    ]
    spans = [
        pltpu.make_async_copy(su_hbm, su_in, span_sem.at[0]),
        pltpu.make_async_copy(sv_hbm, sv_in, span_sem.at[1]),
    ]
    pairs = (
        (u_hbm, u_in), (mu_hbm, mu_in), (eu_hbm, eu_in),
        (v_hbm, v_in), (mv_hbm, mv_in), (ev_hbm, ev_in),
    )
    loads = [
        [
            pltpu.make_async_copy(
                a.at[pl.ds(c * depth, depth)], b.at[pl.ds(c * depth, depth)], load_sem.at[c, k]
            )
            for k, (a, b) in enumerate(pairs)
        ]
        for c in range(chunks)
    ]
    for copy in spans + edges:
        copy.start()
    for per_chunk in loads:
        for copy in per_chunk:
            copy.start()

    barrier = pltpu.get_barrier_semaphore()

    def greet(where):
        pl.semaphore_signal(barrier, inc=1, device_id=where, device_id_type=MESH)

    greet((lat, right))
    if nlon > 2:
        greet((lat, left))

    @pl.when(has_up)
    def _():
        greet((lat + 1, lon))
        greet((lat + 1, left))

    @pl.when(has_down)
    def _():
        greet((lat - 1, lon))
        greet((lat - 1, right))

    if nlon > 3:
        @pl.when(lat == nlat - 1)
        def _():
            for d in range(2, nlon - 1):
                greet((lat, lax.rem(lon + d, nlon)))

    def arrive():
        @pl.when(lat == 0)
        def _():
            pl.semaphore_wait(barrier, sides + 2)

        @pl.when(has_up & has_down)
        def _():
            pl.semaphore_wait(barrier, sides + 4)

        @pl.when(lat == nlat - 1)
        def _():
            pl.semaphore_wait(barrier, sides + 2 + max(nlon - 3, 0))

    def remote(src, dst, send, recv, where):
        return pltpu.make_async_remote_copy(
            src_ref=src, dst_ref=dst, send_sem=send, recv_sem=recv,
            device_id=where, device_id_type=MESH,
        )

    def up_copy():
        return remote(high_own.at[pl.ds(0, 5)], up_in, up_send, up_recv, (lat + 1, lon))

    def down_copy():
        return remote(low_own, down_in, down_send, down_recv, (lat - 1, lon))

    def lon_copies(c):
        return [
            remote(
                pack_own.at[k, c], pack_in.at[k, c],
                lon_send.at[c, k], lon_recv.at[c, k], (lat, target),
            )
            for k, target in enumerate((right, left))
        ]

    def side_copies():
        return [
            remote(edge_own, edge_in.at[k], side_send.at[k], side_recv.at[k], (lat, target))
            for k, target in enumerate((right, left))
        ]

    def corner_down():
        return remote(
            corner_u_own, corner_u, diag_send.at[0], diag_recv.at[0], (lat - 1, right)
        )

    def corner_up():
        return remote(
            corner_v_own, corner_v, diag_send.at[1], diag_recv.at[1], (lat + 1, left)
        )

    def band_copy(d):
        return remote(
            high_own, band.at[lon], band_send.at[d], band_recv.at[d],
            (lat, lax.rem(lon + d, nlon)),
        )

    def band_arrival(d):
        origin = lax.rem(lon + nlon - d, nlon)
        return remote(
            high_own, band.at[origin], band_send.at[d], band_recv.at[d],
            (lat, lax.rem(lon + d, nlon)),
        )

    lane = lax.broadcasted_iota(jnp.int32, (group, lanes), 1)
    sub = lax.broadcasted_iota(jnp.int32, (group, lanes), 0)
    zero = jnp.zeros((group, lanes), f32)

    def clear(l, carry):
        for ref in (um_n, vm_n):
            ref[pl.ds(pl.multiple_of(l * pitch, group), group), :] = zero
        return carry

    lax.fori_loop(0, levels + 1, clear, 0)

    @pl.when(lat == 0)
    def _():
        up_in[...] = jnp.zeros((5, levels, lanes), f32)
        corner_v[...] = zero

    for copy in spans + edges:
        copy.wait()

    def edge_step(g, carry):
        part = pl.ds(pl.multiple_of(g * group, group), group)
        um, vm, tu, tv = [], [], [], []
        for e, r in enumerate(picked):
            mu = edge_m[0, e, part, :].astype(f32)
            mv = edge_m[1, e, part, :].astype(f32)
            um.append(mu * edge_f[0, e, part, :])
            vm.append(mv * edge_f[1, e, part, :])
            vol_u = su_in[pl.ds(r, 1), :] * edge_f[2, e, part, :]
            vol_v = sv_in[pl.ds(r, 1), :] * edge_f[3, e, part, :]
            tu.append(vol_u * um[e])
            tv.append(vol_v * vm[e])
            keep[e, part, :] = mu * scale / vol_u
            keep[4 + e, part, :] = mv * scale / vol_v
        for k, x in enumerate((um[0], um[1], vm[0], vm[1], tu[0], tv[0])):
            low_own[k, part, :] = x
        for k, x in enumerate((um[2], um[3], vm[2], vm[3], tv[3], tu[3])):
            high_own[k, part, :] = x
            band[lon, k, part, :] = x
        keep[8, part, :] = tv[1]
        keep[9, part, :] = tv[2]
        return carry

    lax.fori_loop(0, groups, edge_step, 0)
    arrive()

    @pl.when(has_down)
    def _():
        down_copy().start()

    @pl.when(has_up)
    def _():
        up_copy().start()

    @pl.when(lat == nlat - 1)
    def _():
        for d in range(1, nlon):
            band_copy(d).start()

    first, second, ring = zero, zero, zero
    for g in range(groups):
        part = pl.ds(g * group, group)
        first = jnp.where(lane == g, roll(low_own[4, part, :], g + 1), first)
        tv_top = high_own[4, part, :]
        second = jnp.where(lane == g, roll(tv_top, g), second)
        ring = jnp.where(lane // 4 == g, roll(high_own[3, part, :], 4 * g + 2), ring)
        for k, x in enumerate((low_own[5, part, :], keep[9, part, :], tv_top)):
            ring = jnp.where(lane == 64 + 4 * g + k, roll(x, 64 + 4 * g + k), ring)
    corner_u_own[...] = first
    corner_v_own[...] = second
    edge_own[...] = ring
    for copy in side_copies():
        copy.start()

    @pl.when(has_down)
    def _():
        corner_down().start()

    @pl.when(has_up)
    def _():
        corner_up().start()

    def prepare(block, c):
        um_b, vm_b, tu_b, ts_b, tv_b = [], [], [], [], []
        for s in range(per):
            l = block * per + s
            base = pl.multiple_of(l * pitch + pad, group)
            tus = []
            for b in range(tall):
                at = pl.ds(b * group, group)
                mu = mu_in[l, at, :].astype(f32)
                mv = mv_in[l, at, :].astype(f32)
                um = mu * u_in[l, at, :]
                vm = mv * v_in[l, at, :]
                vol_u = su_in[at, :] * eu_in[l, at, :]
                vol_v = sv_in[at, :] * ev_in[l, at, :]
                tv = vol_v * vm
                tus.append(vol_u * um)
                um_n[pl.ds(base + b * group, group), :] = um
                vm_n[pl.ds(base + b * group, group), :] = vm
                tv_n[l, at, :] = tv
                cu_n[l, at, :] = mu * scale / vol_u
                cv_n[l, at, :] = mv * scale / vol_v
                um_b.append(um)
                vm_b.append(vm)
                tv_b.append(tv)
            turned = [vroll(x, -1) for x in tus] + [zero]
            for b in range(tall):
                ts_b.append(tus[b] + jnp.where(sub == group - 1, turned[b + 1], turned[b]))
            tu_b += tus
        here = block - c * blocks_in
        own = pl.ds(here, 1)

        def flip(tiles):
            return jnp.concatenate(tiles, axis=0).T

        for x, ref, west, east in (
            (flip(um_b), um_t, 0, 0), (flip(vm_b), vm_t, 2, 2),
        ):
            ref[block, pl.ds(pad, lanes), :] = x
            for k in range(2):
                pack_own[0, c, west + k, own, :] = x[lanes - 2 + k:lanes - 1 + k]
                pack_own[1, c, east + k, own, :] = x[k:k + 1]
        x = flip(tu_b)
        tu_t[block, pl.ds(pad, lanes), :] = x
        pack_own[0, c, 4, own, :] = x[lanes - 1:]
        pack_own[1, c, 4, own, :] = x[:1]
        x = flip(ts_b)
        ts_t[block, pl.ds(pad, lanes), :] = x
        pack_own[0, c, 5, own, :] = x[lanes - 1:]
        pack_own[1, c, 5, own, :] = flip(tv_b)[:1]

    def inside(block):
        for s in range(per):
            l = block * per + s
            base = l * pitch + pad

            def um(b, shift):
                return um_n[pl.ds(base + b * group + shift, group), :]

            def vm(b, shift):
                return vm_n[pl.ds(base + b * group + shift, group), :]

            f, w, tv_turned = [], [], []
            for b in range(tall):
                at = pl.ds(b * group, group)
                tv = tv_n[l, at, :]
                tv_turned.append(vroll(tv, 1))
                below = jnp.where(sub == 0, tv_turned[b - 1] if b else zero, tv_turned[b])
                f.append((tv + roll(tv, -1)) * q(um(b, -1), um(b, 0), um(b, 1), um(b, 2)))
                cross = (below + tv) * q(vm(b, -2), vm(b, -1), vm(b, 0), vm(b, 1))
                w.append(jnp.where(sub == 0, 0.0, cross) if b == 0 else cross)
            f_turned = [vroll(x, 1) for x in f]
            w_turned = [vroll(x, -1) for x in w] + [zero]
            for b in range(tall):
                at = pl.ds(b * group, group)
                below = jnp.where(sub == 0, f_turned[b - 1] if b else zero, f_turned[b])
                above = jnp.where(sub == group - 1, w_turned[b + 1], w_turned[b])
                u_part[l, at, :] = um(b, 0) + cu_n[l, at, :] * (f[b] - below)
                v_part[l, at, :] = vm(b, 0) + cv_n[l, at, :] * (above - w[b])

    slot = lax.broadcasted_iota(jnp.int32, (blocks_in, lanes), 1) % rows

    def lane_fix(c):
        own = pack_own[0, c, 1]

        def shifted(x, by):
            keep_it = (slot + by >= 0) & (slot + by < rows)
            return jnp.where(keep_it, pltpu.roll(x, (-by) % lanes, 1), 0.0)

        flux = (pack_in[1, c, 5] - pack_own[1, c, 5]) * q(
            shifted(own, -1), own, shifted(own, 1), shifted(own, 2)
        )
        fix[c] = flux - shifted(flux, -1)

    def across(block, c):
        here = pl.ds(block - c * blocks_in, 1)
        for ref, at in ((um_t, 0), (vm_t, 2)):
            for k in range(2):
                ref[block, pl.ds(pad - 2 + k, 1), :] = pack_in[0, c, at + k, here, :]
                ref[block, pl.ds(pad + lanes + k, 1), :] = pack_in[1, c, at + k, here, :]
        tu_t[block, pl.ds(pad - 1, 1), :] = pack_in[0, c, 4, here, :]
        tu_t[block, pl.ds(pad + lanes, 1), :] = pack_in[1, c, 4, here, :]
        ts_t[block, pl.ds(pad - 1, 1), :] = pack_in[0, c, 5, here, :]

        def read(ref, i):
            return ref[block, pl.ds(pad + i, group), :]

        def west(i):
            return (read(tu_t, i - 1) + read(tu_t, i)) * q(*[read(um_t, i + k) for k in (-2, -1, 0, 1)])

        def east(i):
            return read(ts_t, i) * q(*[read(vm_t, i + k) for k in (-1, 0, 1, 2)])

        count = lanes // group
        fs = [west(i * group) for i in range(count)]
        gs = [east(i * group) for i in range(count)]
        f_turned = [vroll(x, -1) for x in fs] + [west(lanes - group + 1)]
        g_turned = [east(-1)] + [vroll(x, 1) for x in gs]
        du = [
            jnp.where(sub == group - 1, f_turned[i + 1], f_turned[i]) - fs[i] for i in range(count)
        ]
        dv = [gs[i] - jnp.where(sub == 0, g_turned[i], g_turned[i + 1]) for i in range(count)]
        du[-1] = du[-1] + jnp.where(sub == group - 1, fix[c, here, :], 0.0)
        du = jnp.concatenate(du, axis=0).T
        dv = jnp.concatenate(dv, axis=0).T
        for s in range(per):
            l = block * per + s
            for b in range(tall):
                at = pl.ds(b * group, group)
                k = (s * tall + b) * group
                u_part[l, at, :] = u_part[l, at, :] + cu_n[l, at, :] * du[k:k + group]
                v_part[l, at, :] = v_part[l, at, :] + cv_n[l, at, :] * dv[k:k + group]

    def every(body, c):
        def run(i, carry):
            body(i)
            return carry

        lax.fori_loop(c * blocks_in, (c + 1) * blocks_in, run, 0)

    for c in range(chunks):
        for copy in loads[c]:
            copy.wait()
        every(lambda i: prepare(i, c), c)
        for copy in lon_copies(c):
            copy.start()
    for c in range(chunks):
        every(inside, c)

    for copy in side_copies():
        copy.wait()
    for g in range(groups):
        part = pl.ds(g * group, group)
        from_left, from_right = edge_in[0], edge_in[1]
        for k, x in enumerate((low_own[5, part, :], keep[9, part, :], high_own[4, part, :])):
            halo = roll(from_right, -(64 + 4 * g + k))
            side[k, part, :] = x + roll(jnp.where(lane == 0, halo, x), -1)
        vm = high_own[3, part, :]
        halo = roll(jnp.where(lane % 4 < 2, from_left, from_right), -(4 * g + 2))
        w2 = roll(jnp.where(lane >= lanes - 2, halo, vm), 2)
        w1 = roll(jnp.where(lane == lanes - 1, halo, vm), 1)
        e1 = roll(jnp.where(lane == 0, halo, vm), -1)
        e2 = roll(jnp.where(lane < 2, halo, vm), -2)
        side[3, part, :] = q(w2, w1, vm, e1)
        side[4, part, :] = q(w1, vm, e1, e2)

    for c in range(chunks):
        for copy in lon_copies(c):
            copy.wait()
        lane_fix(c)
        every(lambda i: across(i, c), c)

    @pl.when(has_down)
    def _():
        down_copy().wait_send()
        corner_down().wait_send()
        up_copy().wait_recv()
        corner_up().wait_recv()

    @pl.when(has_up)
    def _():
        up_copy().wait_send()
        corner_up().wait_send()
        down_copy().wait_recv()
        corner_down().wait_recv()

    @pl.when(lat == nlat - 1)
    def _():
        for d in range(1, nlon):
            band_copy(d).wait_send()
            band_arrival(d).wait_recv()


def finish_kernel(
    nlat, nlon, levels, rows,
    fold_ref, u_part, v_part, low_own, high_own, keep, side, up_in, down_in, corner_u, corner_v, band,
    u_out, v_out,
    high, high_left, u_low, u_high, v_low, v_high, sem,
):
    lat = lax.axis_index("lat")
    lon = lax.axis_index("lon")
    groups = levels // group
    width = nlon * lanes
    lane = lax.broadcasted_iota(jnp.int32, (group, lanes), 1)
    middle = pl.ds(group, rows - 2 * group)
    low = pl.ds(0, group)
    top = pl.ds(rows - group, group)
    first = [
        pltpu.make_async_copy(a.at[:, middle], b.at[:, middle], sem.at[k])
        for k, (a, b) in enumerate(((u_part, u_out), (v_part, v_out)))
    ]
    for copy in first:
        copy.start()

    @pl.when(lat == nlat - 1)
    def _():
        start = fold_ref[0]
        own = lax.rem(start - lon * lanes - lane + 2 * width, width)
        before = jnp.zeros_like(lane) + lax.rem(start - lon * lanes + 1 + 2 * width, width)

        def pick(k, part, index):
            block = index // lanes
            spot = index % lanes
            got = jnp.zeros((group, lanes), f32)
            for b in range(nlon):
                taken = jnp.take_along_axis(
                    band[b, k, part, :], spot, axis=1, mode="promise_in_bounds"
                )
                got = jnp.where(block == b, taken, got)
            return -got

        for g in range(groups):
            part = pl.ds(g * group, group)
            for k, source in enumerate((1, 0, 3, 2, 5, 4)):
                high[k, part, :] = pick(source, part, own)
            high_left[part, :] = pick(5, part, before)

    @pl.when(lat < nlat - 1)
    def _():
        for g in range(groups):
            part = pl.ds(g * group, group)
            for k in range(6):
                high[k, part, :] = down_in[k, part, :]
            high_left[part, :] = roll(corner_u[...], lanes - 1 - g)

    def copy_tiles(l, carry):
        for source, a, b in ((u_part, u_low, u_high), (v_part, v_low, v_high)):
            a[l] = source[l, low, :]
            b[l] = source[l, top, :]
        return carry

    lax.fori_loop(0, levels, copy_tiles, 0, unroll=8)

    views = [ref.reshape(levels * group, lanes) for ref in (u_low, u_high, v_low, v_high)]

    def add(view, g, row, value):
        at = pl.ds(g * group * group + row, group, stride=group)
        view[at, :] = view[at, :] + value

    for g in range(groups):
        part = pl.ds(g * group, group)
        um0, um1, vm0, vm1, _, tv0 = [low_own[k, part, :] for k in range(6)]
        vm30, vm31, tv31 = [high_own[k, part, :] for k in (2, 3, 4)]
        um_2, um_1, vm_2, vm_1, tv_1 = [up_in[k, part, :] for k in range(5)]
        um32, um33, vm32, vm33, tu32, tv32 = [high[k, part, :] for k in range(6)]
        cu0, cu1, cu30, cu31, cv0, cv1, cv30, cv31, tv1, tv30 = [keep[k, part, :] for k in range(10)]
        v0, v30, v31, q_west, q_east = [side[k, part, :] for k in range(5)]

        face = tv_1 + roll(jnp.where(lane == 0, roll(corner_v[...], -g), tv_1), -1)
        f_low = face * q(um_2, um_1, um0, um1)
        d0 = v0 * um_1
        add(views[0], g, 0, -cu0 * (d0 + f_low))
        add(views[0], g, 1, cu1 * d0)
        w_low = (tv_1 + tv0) * q(vm_2, vm_1, vm0, vm1)
        d0 = (tv0 + tv1) * vm_1
        add(views[2], g, 0, -cv0 * (d0 + w_low))
        add(views[2], g, 1, cv1 * d0)
        d30 = v30 * um32
        add(views[1], g, group - 2, -cu30 * d30)
        add(views[1], g, group - 1, cu31 * (v31 * (7.0 * um32 - um33) + d30))
        d30 = (tv30 + tv31) * vm32
        w_high = (tv31 + tv32) * q(vm30, vm31, vm32, vm33)
        tu_west = roll(jnp.where(lane == lanes - 1, high_left[part, :], tu32), 1)
        add(views[3], g, group - 2, -cv30 * d30)
        add(views[3], g, group - 1, cv31 * (w_high + d30 + (tu32 * q_east - tu_west * q_west)))

    last = [
        pltpu.make_async_copy(a, b.at[:, at], sem.at[2 + k])
        for k, (a, b, at) in enumerate((
            (u_low, u_out, low), (u_high, u_out, top), (v_low, v_out, low), (v_high, v_out, top),
        ))
    ]
    for copy in last:
        copy.start()
    for copy in first + last:
        copy.wait()


def local(nlat, nlon, u, v, eu, ev, su, sv, mu, mv, fold):
    u, v, eu, ev, su, sv, mu, mv = [
        pltpu.with_memory_space_constraint(x, pltpu.HBM) for x in (u, v, eu, ev, su, sv, mu, mv)
    ]
    levels, rows, _ = u.shape
    per = lanes // rows
    blocks = levels // per
    chunks = chunk_count(levels, per)
    blocks_in = blocks // chunks
    pitch = rows + pad
    vmem = pl.BlockSpec(memory_space=pltpu.VMEM)
    hbm = pl.BlockSpec(memory_space=pltpu.HBM)
    block = (levels, rows, lanes)
    line = (levels, lanes)
    shapes = [
        block, block,
        (6,) + line, (6,) + line, (10,) + line, (5,) + line, (5,) + line, (6,) + line,
        (group, lanes), (group, lanes), (nlon, 6) + line,
    ]
    tall = (levels * pitch + pad, lanes)
    turned = (blocks, lanes + 2 * pad, lanes)
    packs = (2, chunks, 6, blocks_in, lanes)
    dma = pltpu.SemaphoreType.DMA
    V = pltpu.VMEM
    fields = pl.pallas_call(
        functools.partial(exchange_kernel, nlat, nlon, levels, rows),
        out_shape=[V(s, f32) for s in shapes],
        in_specs=[hbm] * 8,
        out_specs=[vmem] * len(shapes),
        scratch_shapes=[
            V(block, f32), V(block, f32), V(block, f32), V(block, f32),
            V((rows, lanes), f32), V((rows, lanes), f32),
            V(block, jnp.int32), V(block, jnp.int32),
            V((4, 4) + line, f32), V((2, 4) + line, jnp.int32),
            V(tall, f32), V(tall, f32), V(block, f32), V(block, f32), V(block, f32),
            V(turned, f32), V(turned, f32), V(turned, f32), V(turned, f32),
            V(packs, f32), V(packs, f32),
            V((group, lanes), f32), V((2, group, lanes), f32),
            V((group, lanes), f32), V((group, lanes), f32),
            V((chunks, blocks_in, lanes), f32),
            dma((24,)), dma((chunks, 6)), dma((2,)),
            dma, dma, dma, dma,
            dma((chunks, 2)), dma((chunks, 2)), dma((2,)), dma((2,)), dma((2,)), dma((2,)),
            dma((nlon,)), dma((nlon,)),
        ],
        compiler_params=pltpu.CompilerParams(
            collective_id=0, has_side_effects=True, vmem_limit_bytes=36 * 1024 * 1024
        ),
        name="exchange",
    )(u, v, eu, ev, su, sv, mu, mv)
    strip = (levels, group, lanes)
    result = pl.pallas_call(
        functools.partial(finish_kernel, nlat, nlon, levels, rows),
        out_shape=[jax.ShapeDtypeStruct(block, f32)] * 2,
        in_specs=[pl.BlockSpec(memory_space=pltpu.SMEM)] + [vmem] * len(shapes),
        out_specs=[hbm] * 2,
        scratch_shapes=[
            V((6,) + line, f32), V(line, f32),
            V(strip, f32), V(strip, f32), V(strip, f32), V(strip, f32),
            dma((6,)),
        ],
        compiler_params=pltpu.CompilerParams(vmem_limit_bytes=16 * 1024 * 1024),
        name="finish",
    )(fold, *fields)
    return tuple(result)


def solution(mesh):
    level_rows_columns = P(None, "lat", "lon")
    return jax.shard_map(
        functools.partial(local, mesh.shape["lat"], mesh.shape["lon"]),
        mesh=mesh,
        in_specs=(
            level_rows_columns,
            level_rows_columns,
            level_rows_columns,
            level_rows_columns,
            P("lat", "lon"),
            P("lat", "lon"),
            level_rows_columns,
            level_rows_columns,
            P(),
        ),
        out_specs=(level_rows_columns,) * 2,
        check_vma=False,
    )
```

time: 22.4 us -> 16.3 us (0.73)
  Pallas kernels: 21.6 us -> 15.5 us
    pallas_call x1, Pallas kernels: 10.3 us -> 2.15 us  [local(): pl.pallas_call(functools.partial(finish_kernel, nlat, nlon, levels, rows)...]
    pallas_call x1, Pallas kernels: 11.2 us -> 13.4 us  [local(): pl.pallas_call(functools.partial(exchange_kernel, nlat, nlon, levels, row...]
where the time goes in v1:
time: 16.3 us; the launch traced here: 16.2 us
  Pallas kernels  15.5 us (95%)
  between operations  0.66 us (4%)
    pallas_call x1, Pallas kernels, local(): pl.pallas_call(functools.partial(exchange_kernel, nlat, nlon, levels, row...  13.4 us
    pallas_call x1, Pallas kernels, local(): pl.pallas_call(functools.partial(finish_kernel, nlat, nlon, levels, rows)...  2.15 us

profile of v1, /device:TPU:29, one launch (start us, length us, event | category | flops | bytes accessed | tf_op | source)
XLA Modules:
  0.0 16.2 jit_solution(4981023008467072811)
XLA Ops:
  0.6 0.0 copy-start
  0.6 13.4 %exchange.1 = (f32[72,32,128]{2,1,0:T(8,128)S(1)}, f32[72,32,128]{2,1,0:T(8,128)S(1)}, f32[6,72,128]{2,1,0:T(8,128)S(1)}, f32[6,72,128]{2,1,0:T(8,128)S(1)}, f32...) custom-call(f32[72,32,128]{2,1,0:T(8,128)} %u_hbm.1, ...), custom_call_target="tpu_custom_call" | custom-call | tf_op jit(solution)/shard_map/exchange/pallas_call | solution.py:584
  14.0 0.0 copy-done
  14.0 2.2 %finish.1 = (f32[72,32,128]{2,1,0:T(8,128)}, f32[72,32,128]{2,1,0:T(8,128)}) custom-call(s32[256]{0:T(256)S(1)} %copy-done, f32[72,32,128]{2,1,0:T(8,128)S(1)} %get-tuple-element.13.u_part, f32[72,32,128]{2,1,0:T(8,128)S(1)} %get-tuple-element.14.v_part, f32[6,72,128]{2,1,0:T(8,128)S(1)} %get-tuple-element.15.low_own, ...), custom_call_target="tpu_custom_call" | custom-call | tf_op jit(solution)/shard_map/finish/pallas_call | solution.py:611
Async XLA Ops:
  0.6 13.4 %copy-start = (s32[256]{0:T(256)S(1)}, s32[256]{0:T(256)}, u32[]{:S(2)}) copy-start(s32[256]{0:T(256)} %fold_ref.1) | copy-start | bytes 3076

commit v2 on v1

--- a/solution.py
+++ b/solution.py
@@ -18,7 +18,7 @@
 
 def chunk_count(levels, per):
     count = levels // per
-    return next(c for c in (3, 2, 1) if count % c == 0)
+    return next(c for c in (6, 3, 2, 1) if count % c == 0)
 
 
 def roll(x, shift):
@@ -51,6 +51,8 @@
     blocks_in = blocks // chunks
     groups = levels // group
     pitch = rows + pad
+    step = next(n for n in (3, 2, 1) if blocks_in % n == 0)
+    ahead = 2
     lat = lax.axis_index("lat")
     lon = lax.axis_index("lon")
     right = lax.rem(lon + 1, nlon)
@@ -87,9 +89,14 @@
     ]
     for copy in spans + edges:
         copy.start()
-    for per_chunk in loads:
-        for copy in per_chunk:
-            copy.start()
+
+    def fetch(c):
+        if c < chunks:
+            for copy in loads[c]:
+                copy.start()
+
+    for c in range(ahead):
+        fetch(c)
 
     barrier = pltpu.get_barrier_semaphore()
 
@@ -166,18 +173,27 @@
             corner_v_own, corner_v, diag_send.at[1], diag_recv.at[1], (lat + 1, left)
         )
 
-    def band_copy(d):
+    def band_copy(d, k):
         return remote(
-            high_own, band.at[lon], band_send.at[d], band_recv.at[d],
+            high_own.at[k], band.at[lon, k], band_send.at[d, k], band_recv.at[d, k],
             (lat, lax.rem(lon + d, nlon)),
         )
 
-    def band_arrival(d):
+    def band_arrival(d, k):
         origin = lax.rem(lon + nlon - d, nlon)
         return remote(
-            high_own, band.at[origin], band_send.at[d], band_recv.at[d],
+            high_own.at[k], band.at[origin, k], band_send.at[d, k], band_recv.at[d, k],
             (lat, lax.rem(lon + d, nlon)),
         )
+
+    stages = chunks + 1
+
+    def send_band(stage):
+        @pl.when(lat == nlat - 1)
+        def _():
+            for k in range(6 * stage // stages, 6 * (stage + 1) // stages):
+                for d in range(1, nlon):
+                    band_copy(d, k).start()
 
     lane = lax.broadcasted_iota(jnp.int32, (group, lanes), 1)
     sub = lax.broadcasted_iota(jnp.int32, (group, lanes), 0)
@@ -197,6 +213,7 @@
 
     for copy in spans + edges:
         copy.wait()
+    fetch(ahead)
 
     def edge_step(g, carry):
         part = pl.ds(pl.multiple_of(g * group, group), group)
@@ -232,10 +249,7 @@
     def _():
         up_copy().start()
 
-    @pl.when(lat == nlat - 1)
-    def _():
-        for d in range(1, nlon):
-            band_copy(d).start()
+    send_band(0)
 
     first, second, ring = zero, zero, zero
     for g in range(groups):
@@ -309,6 +323,7 @@
         ts_t[block, pl.ds(pad, lanes), :] = x
         pack_own[0, c, 5, own, :] = x[lanes - 1:]
         pack_own[1, c, 5, own, :] = flip(tv_b)[:1]
+        inside(block)
 
     def inside(block):
         for s in range(per):
@@ -394,19 +409,20 @@
 
     def every(body, c):
         def run(i, carry):
-            body(i)
+            for k in range(step):
+                body(i * step + k)
             return carry
 
-        lax.fori_loop(c * blocks_in, (c + 1) * blocks_in, run, 0)
+        lax.fori_loop(c * blocks_in // step, (c + 1) * blocks_in // step, run, 0)
 
     for c in range(chunks):
         for copy in loads[c]:
             copy.wait()
+        fetch(c + ahead + 1)
         every(lambda i: prepare(i, c), c)
         for copy in lon_copies(c):
             copy.start()
-    for c in range(chunks):
-        every(inside, c)
+        send_band(c + 1)
 
     for copy in side_copies():
         copy.wait()
@@ -448,8 +464,9 @@
     @pl.when(lat == nlat - 1)
     def _():
         for d in range(1, nlon):
-            band_copy(d).wait_send()
-            band_arrival(d).wait_recv()
+            for k in range(6):
+                band_copy(d, k).wait_send()
+                band_arrival(d, k).wait_recv()
 
 
 def finish_kernel(
@@ -600,7 +617,7 @@
             dma((24,)), dma((chunks, 6)), dma((2,)),
             dma, dma, dma, dma,
             dma((chunks, 2)), dma((chunks, 2)), dma((2,)), dma((2,)), dma((2,)), dma((2,)),
-            dma((nlon,)), dma((nlon,)),
+            dma((nlon, 6)), dma((nlon, 6)),
         ],
         compiler_params=pltpu.CompilerParams(
             collective_id=0, has_side_effects=True, vmem_limit_bytes=36 * 1024 * 1024

time: 16.3 us -> 14 us (0.86)
  the two profiles are of different devices: /device:TPU:29 before, /device:TPU:0 now
where the time goes in v2:
time: 14 us; the launch traced here: 13.8 us
  Pallas kernels  13.2 us (94%)
  between operations  0.66 us (5%)
    pallas_call x1, Pallas kernels, local(): pl.pallas_call(functools.partial(exchange_kernel, nlat, nlon, levels, row...  11.2 us
    pallas_call x1, Pallas kernels, local(): pl.pallas_call(functools.partial(finish_kernel, nlat, nlon, levels, rows)...  2 us

profile of v2, /device:TPU:0, one launch (start us, length us, event | category | flops | bytes accessed | tf_op | source)
XLA Modules:
  0.0 13.8 jit_solution(8852018041344484343)
XLA Ops:
  0.6 0.0 copy-start
  0.6 11.2 %exchange.1 = (f32[72,32,128]{2,1,0:T(8,128)S(1)}, f32[72,32,128]{2,1,0:T(8,128)S(1)}, f32[6,72,128]{2,1,0:T(8,128)S(1)}, f32[6,72,128]{2,1,0:T(8,128)S(1)}, f32...) custom-call(f32[72,32,128]{2,1,0:T(8,128)} %u_hbm.1, ...), custom_call_target="tpu_custom_call" | custom-call | tf_op jit(solution)/shard_map/exchange/pallas_call | solution.py:601
  11.8 0.0 copy-done
  11.8 2.0 %finish.1 = (f32[72,32,128]{2,1,0:T(8,128)}, f32[72,32,128]{2,1,0:T(8,128)}) custom-call(s32[256]{0:T(256)S(1)} %copy-done, f32[72,32,128]{2,1,0:T(8,128)S(1)} %get-tuple-element.13.u_part, f32[72,32,128]{2,1,0:T(8,128)S(1)} %get-tuple-element.14.v_part, f32[6,72,128]{2,1,0:T(8,128)S(1)} %get-tuple-element.15.low_own, ...), custom_call_target="tpu_custom_call" | custom-call | tf_op jit(solution)/shard_map/finish/pallas_call | solution.py:628
Async XLA Ops:
  0.6 11.2 %copy-start = (s32[256]{0:T(256)S(1)}, s32[256]{0:T(256)}, u32[]{:S(2)}) copy-start(s32[256]{0:T(256)} %fold_ref.1) | copy-start | bytes 3076

commit v3 on v2

--- a/solution.py
+++ b/solution.py
@@ -37,66 +37,56 @@
     nlat, nlon, levels, rows,
     u_hbm, v_hbm, eu_hbm, ev_hbm, su_hbm, sv_hbm, mu_hbm, mv_hbm,
     u_part, v_part, low_own, high_own, keep, side, up_in, down_in, corner_u, corner_v, band,
-    u_in, v_in, eu_in, ev_in, su_in, sv_in, mu_in, mv_in,
+    real_in, mask_in, span_in,
     edge_f, edge_m, um_n, vm_n, tv_n, cu_n, cv_n, um_t, vm_t, tu_t, ts_t,
-    pack_own, pack_in, edge_own, edge_in, corner_u_own, corner_v_own, fix,
-    edge_sem, load_sem, span_sem, up_send, up_recv, down_send, down_recv,
+    pack_own, pack_in, edge_own, edge_in, fix,
+    early_sem, load_sem, up_send, up_recv, down_send, down_recv,
     lon_send, lon_recv, side_send, side_recv, diag_send, diag_recv, band_send, band_recv,
 ):
     per = lanes // rows
     tall = rows // group
     blocks = levels // per
     chunks = chunk_count(levels, per)
-    depth = levels // chunks
     blocks_in = blocks // chunks
     groups = levels // group
     pitch = rows + pad
     step = next(n for n in (3, 2, 1) if blocks_in % n == 0)
-    ahead = 2
+    loads = 3 if chunks % 3 == 0 else chunks
+    depth = levels // loads
     lat = lax.axis_index("lat")
     lon = lax.axis_index("lon")
     right = lax.rem(lon + 1, nlon)
     left = lax.rem(lon + nlon - 1, nlon)
     has_up = lat < nlat - 1
     has_down = lat > 0
-    sides = 1 if nlon == 2 else 2
+    targets = (right,) if nlon == 2 else (right, left)
+    sides = len(targets)
     picked = (0, 1, rows - 2, rows - 1)
 
-    edges = [
-        pltpu.make_async_copy(a.at[:, r, :], b.at[k, e], edge_sem.at[4 * s + e])
-        for s, (a, b, k) in enumerate((
-            (u_hbm, edge_f, 0), (mu_hbm, edge_m, 0), (v_hbm, edge_f, 1),
-            (mv_hbm, edge_m, 1), (eu_hbm, edge_f, 2), (ev_hbm, edge_f, 3),
-        ))
-        for e, r in enumerate(picked)
-    ]
-    spans = [
-        pltpu.make_async_copy(su_hbm, su_in, span_sem.at[0]),
-        pltpu.make_async_copy(sv_hbm, sv_in, span_sem.at[1]),
-    ]
-    pairs = (
-        (u_hbm, u_in), (mu_hbm, mu_in), (eu_hbm, eu_in),
-        (v_hbm, v_in), (mv_hbm, mv_in), (ev_hbm, ev_in),
-    )
-    loads = [
-        [
-            pltpu.make_async_copy(
-                a.at[pl.ds(c * depth, depth)], b.at[pl.ds(c * depth, depth)], load_sem.at[c, k]
-            )
-            for k, (a, b) in enumerate(pairs)
-        ]
-        for c in range(chunks)
-    ]
-    for copy in spans + edges:
-        copy.start()
-
-    def fetch(c):
-        if c < chunks:
-            for copy in loads[c]:
-                copy.start()
-
-    for c in range(ahead):
-        fetch(c)
+    reals = (u_hbm, v_hbm, eu_hbm, ev_hbm)
+    masks = (mu_hbm, mv_hbm)
+
+    def fetch_edges(sources, edge, sem):
+        for k, source in enumerate(sources):
+            for e, r in enumerate(picked):
+                pltpu.make_async_copy(source.at[:, r, :], edge.at[k, e], sem).start()
+
+    def fetch_part(c):
+        part = pl.ds(c * depth, depth)
+        for k, source in enumerate(reals):
+            pltpu.make_async_copy(source.at[part], real_in.at[k, part], load_sem.at[c, 0]).start(priority=1)
+        for k, source in enumerate(masks):
+            pltpu.make_async_copy(source.at[part], mask_in.at[k, part], load_sem.at[c, 1]).start(priority=1)
+
+    def landed(ref, sem):
+        pltpu.make_async_copy(ref, ref, sem).wait()
+
+    fetch_edges(reals, edge_f, early_sem.at[0])
+    fetch_edges(masks, edge_m, early_sem.at[1])
+    pltpu.make_async_copy(su_hbm, span_in.at[0], early_sem.at[2]).start()
+    pltpu.make_async_copy(sv_hbm, span_in.at[1], early_sem.at[2]).start()
+    for c in range(loads):
+        fetch_part(c)
 
     barrier = pltpu.get_barrier_semaphore()
 
@@ -110,12 +100,10 @@
     @pl.when(has_up)
     def _():
         greet((lat + 1, lon))
-        greet((lat + 1, left))
 
     @pl.when(has_down)
     def _():
         greet((lat - 1, lon))
-        greet((lat - 1, right))
 
     if nlon > 3:
         @pl.when(lat == nlat - 1)
@@ -126,15 +114,15 @@
     def arrive():
         @pl.when(lat == 0)
         def _():
-            pl.semaphore_wait(barrier, sides + 2)
+            pl.semaphore_wait(barrier, sides + 1)
 
         @pl.when(has_up & has_down)
         def _():
-            pl.semaphore_wait(barrier, sides + 4)
+            pl.semaphore_wait(barrier, sides + 2)
 
         @pl.when(lat == nlat - 1)
         def _():
-            pl.semaphore_wait(barrier, sides + 2 + max(nlon - 3, 0))
+            pl.semaphore_wait(barrier, sides + 1 + max(nlon - 3, 0))
 
     def remote(src, dst, send, recv, where):
         return pltpu.make_async_remote_copy(
@@ -149,40 +137,49 @@
         return remote(low_own, down_in, down_send, down_recv, (lat - 1, lon))
 
     def lon_copies(c):
+        if nlon == 2:
+            return [remote(pack_own.at[:, c], pack_in.at[:, c], lon_send.at[0], lon_recv.at[c, 0], (lat, right))]
         return [
-            remote(
-                pack_own.at[k, c], pack_in.at[k, c],
-                lon_send.at[c, k], lon_recv.at[c, k], (lat, target),
-            )
-            for k, target in enumerate((right, left))
+            remote(pack_own.at[k, c], pack_in.at[k, c], lon_send.at[k], lon_recv.at[c, k], (lat, target))
+            for k, target in enumerate(targets)
+        ]
+
+    def lon_sent():
+        if nlon == 2:
+            return [remote(pack_own, pack_in, lon_send.at[0], lon_recv.at[0, 0], (lat, right))]
+        return [
+            remote(pack_own.at[k], pack_in.at[k], lon_send.at[k], lon_recv.at[0, k], (lat, target))
+            for k, target in enumerate(targets)
         ]
 
     def side_copies():
         return [
             remote(edge_own, edge_in.at[k], side_send.at[k], side_recv.at[k], (lat, target))
-            for k, target in enumerate((right, left))
+            for k, target in enumerate(targets)
         ]
 
     def corner_down():
-        return remote(
-            corner_u_own, corner_u, diag_send.at[0], diag_recv.at[0], (lat - 1, right)
-        )
+        return remote(edge_in.at[0], corner_u, diag_send.at[0], diag_recv.at[0], (lat - 1, lon))
 
     def corner_up():
-        return remote(
-            corner_v_own, corner_v, diag_send.at[1], diag_recv.at[1], (lat + 1, left)
-        )
+        return remote(edge_in.at[sides - 1], corner_v, diag_send.at[1], diag_recv.at[1], (lat + 1, lon))
 
     def band_copy(d, k):
         return remote(
-            high_own.at[k], band.at[lon, k], band_send.at[d, k], band_recv.at[d, k],
+            high_own.at[k], band.at[lon, k], band_send.at[d], band_recv.at[d],
             (lat, lax.rem(lon + d, nlon)),
         )
 
-    def band_arrival(d, k):
+    def band_sent(d):
+        return remote(
+            high_own, band.at[lon], band_send.at[d], band_recv.at[d],
+            (lat, lax.rem(lon + d, nlon)),
+        )
+
+    def band_arrival(d):
         origin = lax.rem(lon + nlon - d, nlon)
         return remote(
-            high_own.at[k], band.at[origin, k], band_send.at[d, k], band_recv.at[d, k],
+            high_own, band.at[origin], band_send.at[d], band_recv.at[d],
             (lat, lax.rem(lon + d, nlon)),
         )
 
@@ -211,9 +208,9 @@
         up_in[...] = jnp.zeros((5, levels, lanes), f32)
         corner_v[...] = zero
 
-    for copy in spans + edges:
-        copy.wait()
-    fetch(ahead)
+    landed(edge_f, early_sem.at[0])
+    landed(edge_m, early_sem.at[1])
+    landed(span_in, early_sem.at[2])
 
     def edge_step(g, carry):
         part = pl.ds(pl.multiple_of(g * group, group), group)
@@ -223,8 +220,8 @@
             mv = edge_m[1, e, part, :].astype(f32)
             um.append(mu * edge_f[0, e, part, :])
             vm.append(mv * edge_f[1, e, part, :])
-            vol_u = su_in[pl.ds(r, 1), :] * edge_f[2, e, part, :]
-            vol_v = sv_in[pl.ds(r, 1), :] * edge_f[3, e, part, :]
+            vol_u = span_in[0, pl.ds(r, 1), :] * edge_f[2, e, part, :]
+            vol_v = span_in[1, pl.ds(r, 1), :] * edge_f[3, e, part, :]
             tu.append(vol_u * um[e])
             tv.append(vol_v * vm[e])
             keep[e, part, :] = mu * scale / vol_u
@@ -251,28 +248,17 @@
 
     send_band(0)
 
-    first, second, ring = zero, zero, zero
+    ring = zero
     for g in range(groups):
         part = pl.ds(g * group, group)
-        first = jnp.where(lane == g, roll(low_own[4, part, :], g + 1), first)
         tv_top = high_own[4, part, :]
-        second = jnp.where(lane == g, roll(tv_top, g), second)
         ring = jnp.where(lane // 4 == g, roll(high_own[3, part, :], 4 * g + 2), ring)
         for k, x in enumerate((low_own[5, part, :], keep[9, part, :], tv_top)):
             ring = jnp.where(lane == 64 + 4 * g + k, roll(x, 64 + 4 * g + k), ring)
-    corner_u_own[...] = first
-    corner_v_own[...] = second
+        ring = jnp.where(lane == 64 + 4 * g + 3, roll(low_own[4, part, :], 64 + 4 * g + 4), ring)
     edge_own[...] = ring
     for copy in side_copies():
         copy.start()
-
-    @pl.when(has_down)
-    def _():
-        corner_down().start()
-
-    @pl.when(has_up)
-    def _():
-        corner_up().start()
 
     def prepare(block, c):
         um_b, vm_b, tu_b, ts_b, tv_b = [], [], [], [], []
@@ -282,12 +268,12 @@
             tus = []
             for b in range(tall):
                 at = pl.ds(b * group, group)
-                mu = mu_in[l, at, :].astype(f32)
-                mv = mv_in[l, at, :].astype(f32)
-                um = mu * u_in[l, at, :]
-                vm = mv * v_in[l, at, :]
-                vol_u = su_in[at, :] * eu_in[l, at, :]
-                vol_v = sv_in[at, :] * ev_in[l, at, :]
+                mu = mask_in[0, l, at, :].astype(f32)
+                mv = mask_in[1, l, at, :].astype(f32)
+                um = mu * real_in[0, l, at, :]
+                vm = mv * real_in[1, l, at, :]
+                vol_u = span_in[0, at, :] * real_in[2, l, at, :]
+                vol_v = span_in[1, at, :] * real_in[3, l, at, :]
                 tv = vol_v * vm
                 tus.append(vol_u * um)
                 um_n[pl.ds(base + b * group, group), :] = um
@@ -416,9 +402,10 @@
         lax.fori_loop(c * blocks_in // step, (c + 1) * blocks_in // step, run, 0)
 
     for c in range(chunks):
-        for copy in loads[c]:
-            copy.wait()
-        fetch(c + ahead + 1)
+        if c * loads % chunks == 0:
+            part = pl.ds(c * loads // chunks * depth, depth)
+            landed(real_in.at[:, part], load_sem.at[c * loads // chunks, 0])
+            landed(mask_in.at[:, part], load_sem.at[c * loads // chunks, 1])
         every(lambda i: prepare(i, c), c)
         for copy in lon_copies(c):
             copy.start()
@@ -426,9 +413,18 @@
 
     for copy in side_copies():
         copy.wait()
+
+    @pl.when(has_down)
+    def _():
+        corner_down().start()
+
+    @pl.when(has_up)
+    def _():
+        corner_up().start()
+
     for g in range(groups):
         part = pl.ds(g * group, group)
-        from_left, from_right = edge_in[0], edge_in[1]
+        from_left, from_right = edge_in[0], edge_in[sides - 1]
         for k, x in enumerate((low_own[5, part, :], keep[9, part, :], high_own[4, part, :])):
             halo = roll(from_right, -(64 + 4 * g + k))
             side[k, part, :] = x + roll(jnp.where(lane == 0, halo, x), -1)
@@ -443,9 +439,12 @@
 
     for c in range(chunks):
         for copy in lon_copies(c):
-            copy.wait()
+            copy.wait_recv()
         lane_fix(c)
         every(lambda i: across(i, c), c)
+
+    for copy in lon_sent():
+        copy.wait_send()
 
     @pl.when(has_down)
     def _():
@@ -464,9 +463,8 @@
     @pl.when(lat == nlat - 1)
     def _():
         for d in range(1, nlon):
-            for k in range(6):
-                band_copy(d, k).wait_send()
-                band_arrival(d, k).wait_recv()
+            band_sent(d).wait_send()
+            band_arrival(d).wait_recv()
 
 
 def finish_kernel(
@@ -519,7 +517,7 @@
             part = pl.ds(g * group, group)
             for k in range(6):
                 high[k, part, :] = down_in[k, part, :]
-            high_left[part, :] = roll(corner_u[...], lanes - 1 - g)
+            high_left[part, :] = roll(corner_u[...], lanes - 68 - 4 * g)
 
     def copy_tiles(l, carry):
         for source, a, b in ((u_part, u_low, u_high), (v_part, v_low, v_high)):
@@ -544,7 +542,7 @@
         cu0, cu1, cu30, cu31, cv0, cv1, cv30, cv31, tv1, tv30 = [keep[k, part, :] for k in range(10)]
         v0, v30, v31, q_west, q_east = [side[k, part, :] for k in range(5)]
 
-        face = tv_1 + roll(jnp.where(lane == 0, roll(corner_v[...], -g), tv_1), -1)
+        face = tv_1 + roll(jnp.where(lane == 0, roll(corner_v[...], -(66 + 4 * g)), tv_1), -1)
         f_low = face * q(um_2, um_1, um0, um1)
         d0 = v0 * um_1
         add(views[0], g, 0, -cu0 * (d0 + f_low))
@@ -583,6 +581,8 @@
     blocks = levels // per
     chunks = chunk_count(levels, per)
     blocks_in = blocks // chunks
+    loads = 3 if chunks % 3 == 0 else chunks
+    sides = 1 if nlon == 2 else 2
     pitch = rows + pad
     vmem = pl.BlockSpec(memory_space=pltpu.VMEM)
     hbm = pl.BlockSpec(memory_space=pltpu.HBM)
@@ -604,20 +604,17 @@
         in_specs=[hbm] * 8,
         out_specs=[vmem] * len(shapes),
         scratch_shapes=[
-            V(block, f32), V(block, f32), V(block, f32), V(block, f32),
-            V((rows, lanes), f32), V((rows, lanes), f32),
-            V(block, jnp.int32), V(block, jnp.int32),
+            V((4,) + block, f32), V((2,) + block, jnp.int32), V((2, rows, lanes), f32),
             V((4, 4) + line, f32), V((2, 4) + line, jnp.int32),
             V(tall, f32), V(tall, f32), V(block, f32), V(block, f32), V(block, f32),
             V(turned, f32), V(turned, f32), V(turned, f32), V(turned, f32),
             V(packs, f32), V(packs, f32),
-            V((group, lanes), f32), V((2, group, lanes), f32),
-            V((group, lanes), f32), V((group, lanes), f32),
+            V((group, lanes), f32), V((sides, group, lanes), f32),
             V((chunks, blocks_in, lanes), f32),
-            dma((24,)), dma((chunks, 6)), dma((2,)),
+            dma((3,)), dma((loads, 2)),
             dma, dma, dma, dma,
-            dma((chunks, 2)), dma((chunks, 2)), dma((2,)), dma((2,)), dma((2,)), dma((2,)),
-            dma((nlon, 6)), dma((nlon, 6)),
+            dma((sides,)), dma((chunks, sides)), dma((sides,)), dma((sides,)), dma((2,)), dma((2,)),
+            dma((nlon,)), dma((nlon,)),
         ],
         compiler_params=pltpu.CompilerParams(
             collective_id=0, has_side_effects=True, vmem_limit_bytes=36 * 1024 * 1024

time: 14 us -> 12.7 us (0.907)
  Pallas kernels: 13.2 us -> 11.9 us
    pallas_call x1, Pallas kernels: 11.2 us -> 9.93 us  [local(): pl.pallas_call(functools.partial(exchange_kernel, nlat, nlon, levels, row...]
where the time goes in v3:
time: 12.7 us; the launch traced here: 12.6 us
  Pallas kernels  11.9 us (94%)
  between operations  0.66 us (5%)
    pallas_call x1, Pallas kernels, local(): pl.pallas_call(functools.partial(exchange_kernel, nlat, nlon, levels, row...  9.93 us
    pallas_call x1, Pallas kernels, local(): pl.pallas_call(functools.partial(finish_kernel, nlat, nlon, levels, rows)...  2 us

profile of v3, /device:TPU:0, one launch (start us, length us, event | category | flops | bytes accessed | tf_op | source)
XLA Modules:
  0.0 12.6 jit_solution(5884940117856564214)
XLA Ops:
  0.6 0.0 copy-start
  0.6 9.9 %exchange.1 = (f32[72,32,128]{2,1,0:T(8,128)S(1)}, f32[72,32,128]{2,1,0:T(8,128)S(1)}, f32[6,72,128]{2,1,0:T(8,128)S(1)}, f32[6,72,128]{2,1,0:T(8,128)S(1)}, f32...) custom-call(f32[72,32,128]{2,1,0:T(8,128)} %u_hbm.1, ...), custom_call_target="tpu_custom_call" | custom-call | tf_op jit(solution)/shard_map/exchange/pallas_call | solution.py:601
  10.6 0.0 copy-done
  10.6 2.0 %finish.1 = (f32[72,32,128]{2,1,0:T(8,128)}, f32[72,32,128]{2,1,0:T(8,128)}) custom-call(s32[256]{0:T(256)S(1)} %copy-done, f32[72,32,128]{2,1,0:T(8,128)S(1)} %get-tuple-element.13.u_part, f32[72,32,128]{2,1,0:T(8,128)S(1)} %get-tuple-element.14.v_part, f32[6,72,128]{2,1,0:T(8,128)S(1)} %get-tuple-element.15.low_own, ...), custom_call_target="tpu_custom_call" | custom-call | tf_op jit(solution)/shard_map/finish/pallas_call | solution.py:625
Async XLA Ops:
  0.6 10.0 %copy-start = (s32[256]{0:T(256)S(1)}, s32[256]{0:T(256)}, u32[]{:S(2)}) copy-start(s32[256]{0:T(256)} %fold_ref.1) | copy-start | bytes 3076

commit v4 on v3

--- a/solution.py
+++ b/solution.py
@@ -36,9 +36,10 @@
 def exchange_kernel(
     nlat, nlon, levels, rows,
     u_hbm, v_hbm, eu_hbm, ev_hbm, su_hbm, sv_hbm, mu_hbm, mv_hbm,
-    u_part, v_part, low_own, high_own, keep, side, up_in, down_in, corner_u, corner_v, band,
+    u_low, u_mid, u_high, v_low, v_mid, v_high,
+    low_own, high_own, keep, side, up_in, down_in, corner_u, corner_v, band,
     real_in, mask_in, span_in,
-    edge_f, edge_m, um_n, vm_n, tv_n, cu_n, cv_n, um_t, vm_t, tu_t, ts_t,
+    edge_f, edge_m, um_n, vm_n, tv_n, cu_n, cv_n, um_t, vm_t, tu_t,
     pack_own, pack_in, edge_own, edge_in, fix,
     early_sem, load_sem, up_send, up_recv, down_send, down_recv,
     lon_send, lon_recv, side_send, side_recv, diag_send, diag_recv, band_send, band_recv,
@@ -136,20 +137,20 @@
     def down_copy():
         return remote(low_own, down_in, down_send, down_recv, (lat - 1, lon))
 
+    cuts = ((pl.ds(0, 11), right),) if nlon == 2 else ((pl.ds(0, 5), right), (pl.ds(5, 6), left))
+
     def lon_copies(c):
-        if nlon == 2:
-            return [remote(pack_own.at[:, c], pack_in.at[:, c], lon_send.at[0], lon_recv.at[c, 0], (lat, right))]
         return [
-            remote(pack_own.at[k, c], pack_in.at[k, c], lon_send.at[k], lon_recv.at[c, k], (lat, target))
-            for k, target in enumerate(targets)
+            remote(pack_own.at[c, cut], pack_in.at[c, cut], lon_send.at[k], lon_recv.at[c, k], (lat, target))
+            for k, (cut, target) in enumerate(cuts)
         ]
 
     def lon_sent():
-        if nlon == 2:
-            return [remote(pack_own, pack_in, lon_send.at[0], lon_recv.at[0, 0], (lat, right))]
         return [
-            remote(pack_own.at[k], pack_in.at[k], lon_send.at[k], lon_recv.at[0, k], (lat, target))
-            for k, target in enumerate(targets)
+            remote(
+                pack_own.at[:, cut], pack_in.at[:, cut], lon_send.at[k], lon_recv.at[0, k], (lat, target)
+            )
+            for k, (cut, target) in enumerate(cuts)
         ]
 
     def side_copies():
@@ -188,20 +189,13 @@
     def send_band(stage):
         @pl.when(lat == nlat - 1)
         def _():
-            for k in range(6 * stage // stages, 6 * (stage + 1) // stages):
+            for k in range(4 * stage // stages + 2 * (stage > 0), 4 * (stage + 1) // stages + 2):
                 for d in range(1, nlon):
                     band_copy(d, k).start()
 
     lane = lax.broadcasted_iota(jnp.int32, (group, lanes), 1)
     sub = lax.broadcasted_iota(jnp.int32, (group, lanes), 0)
     zero = jnp.zeros((group, lanes), f32)
-
-    def clear(l, carry):
-        for ref in (um_n, vm_n):
-            ref[pl.ds(pl.multiple_of(l * pitch, group), group), :] = zero
-        return carry
-
-    lax.fori_loop(0, levels + 1, clear, 0)
 
     @pl.when(lat == 0)
     def _():
@@ -236,18 +230,6 @@
         return carry
 
     lax.fori_loop(0, groups, edge_step, 0)
-    arrive()
-
-    @pl.when(has_down)
-    def _():
-        down_copy().start()
-
-    @pl.when(has_up)
-    def _():
-        up_copy().start()
-
-    send_band(0)
-
     ring = zero
     for g in range(groups):
         part = pl.ds(g * group, group)
@@ -257,15 +239,49 @@
             ring = jnp.where(lane == 64 + 4 * g + k, roll(x, 64 + 4 * g + k), ring)
         ring = jnp.where(lane == 64 + 4 * g + 3, roll(low_own[4, part, :], 64 + 4 * g + 4), ring)
     edge_own[...] = ring
-    for copy in side_copies():
-        copy.start()
+    def forward():
+        for copy in side_copies():
+            copy.wait()
+
+        @pl.when(has_down)
+        def _():
+            corner_down().start()
+
+        @pl.when(has_up)
+        def _():
+            corner_up().start()
+
+    def begin():
+        arrive()
+
+        @pl.when(has_down)
+        def _():
+            down_copy().start()
+
+        @pl.when(has_up)
+        def _():
+            up_copy().start()
+
+        send_band(0)
+
+        for copy in side_copies():
+            copy.start()
+
+    def clear(l, carry):
+        for ref in (um_n, vm_n):
+            ref[pl.ds(pl.multiple_of(l * pitch, group), group), :] = zero
+        return carry
+
+    lax.fori_loop(0, levels, clear, 0, unroll=8)
+    clear(levels, 0)
+
+    begin()
 
     def prepare(block, c):
-        um_b, vm_b, tu_b, ts_b, tv_b = [], [], [], [], []
+        um_b, vm_b, tu_b, tv_b = [], [], [], []
         for s in range(per):
             l = block * per + s
             base = pl.multiple_of(l * pitch + pad, group)
-            tus = []
             for b in range(tall):
                 at = pl.ds(b * group, group)
                 mu = mask_in[0, l, at, :].astype(f32)
@@ -275,7 +291,7 @@
                 vol_u = span_in[0, at, :] * real_in[2, l, at, :]
                 vol_v = span_in[1, at, :] * real_in[3, l, at, :]
                 tv = vol_v * vm
-                tus.append(vol_u * um)
+                tu_b.append(vol_u * um)
                 um_n[pl.ds(base + b * group, group), :] = um
                 vm_n[pl.ds(base + b * group, group), :] = vm
                 tv_n[l, at, :] = tv
@@ -284,32 +300,33 @@
                 um_b.append(um)
                 vm_b.append(vm)
                 tv_b.append(tv)
-            turned = [vroll(x, -1) for x in tus] + [zero]
-            for b in range(tall):
-                ts_b.append(tus[b] + jnp.where(sub == group - 1, turned[b + 1], turned[b]))
-            tu_b += tus
         here = block - c * blocks_in
         own = pl.ds(here, 1)
 
         def flip(tiles):
             return jnp.concatenate(tiles, axis=0).T
 
-        for x, ref, west, east in (
-            (flip(um_b), um_t, 0, 0), (flip(vm_b), vm_t, 2, 2),
-        ):
+        for x, ref, first in ((flip(um_b), um_t, 0), (flip(vm_b), vm_t, 2)):
             ref[block, pl.ds(pad, lanes), :] = x
             for k in range(2):
-                pack_own[0, c, west + k, own, :] = x[lanes - 2 + k:lanes - 1 + k]
-                pack_own[1, c, east + k, own, :] = x[k:k + 1]
+                pack_own[c, first + k, own, :] = x[lanes - 2 + k:lanes - 1 + k]
+                pack_own[c, 5 + first + k, own, :] = x[k:k + 1]
         x = flip(tu_b)
         tu_t[block, pl.ds(pad, lanes), :] = x
-        pack_own[0, c, 4, own, :] = x[lanes - 1:]
-        pack_own[1, c, 4, own, :] = x[:1]
-        x = flip(ts_b)
-        ts_t[block, pl.ds(pad, lanes), :] = x
-        pack_own[0, c, 5, own, :] = x[lanes - 1:]
-        pack_own[1, c, 5, own, :] = flip(tv_b)[:1]
-        inside(block)
+        pack_own[c, 4, own, :] = x[lanes - 1:]
+        pack_own[c, 9, own, :] = x[:1]
+        pack_own[c, 10, own, :] = flip(tv_b)[:1]
+
+    def place(parts, b):
+        low, middle, high = parts
+        if b == 0:
+            return low, pl.ds(0, group)
+        if b == tall - 1:
+            return high, pl.ds(0, group)
+        return middle, pl.ds((b - 1) * group, group)
+
+    u_parts = (u_low, u_mid, u_high)
+    v_parts = (v_low, v_mid, v_high)
 
     def inside(block):
         for s in range(per):
@@ -337,19 +354,21 @@
                 at = pl.ds(b * group, group)
                 below = jnp.where(sub == 0, f_turned[b - 1] if b else zero, f_turned[b])
                 above = jnp.where(sub == group - 1, w_turned[b + 1], w_turned[b])
-                u_part[l, at, :] = um(b, 0) + cu_n[l, at, :] * (f[b] - below)
-                v_part[l, at, :] = vm(b, 0) + cv_n[l, at, :] * (above - w[b])
+                ref, to = place(u_parts, b)
+                ref[l, to, :] = um(b, 0) + cu_n[l, at, :] * (f[b] - below)
+                ref, to = place(v_parts, b)
+                ref[l, to, :] = vm(b, 0) + cv_n[l, at, :] * (above - w[b])
 
     slot = lax.broadcasted_iota(jnp.int32, (blocks_in, lanes), 1) % rows
 
     def lane_fix(c):
-        own = pack_own[0, c, 1]
+        own = pack_own[c, 1]
 
         def shifted(x, by):
             keep_it = (slot + by >= 0) & (slot + by < rows)
             return jnp.where(keep_it, pltpu.roll(x, (-by) % lanes, 1), 0.0)
 
-        flux = (pack_in[1, c, 5] - pack_own[1, c, 5]) * q(
+        flux = (pack_in[c, 10] - pack_own[c, 10]) * q(
             shifted(own, -1), own, shifted(own, 1), shifted(own, 2)
         )
         fix[c] = flux - shifted(flux, -1)
@@ -358,11 +377,10 @@
         here = pl.ds(block - c * blocks_in, 1)
         for ref, at in ((um_t, 0), (vm_t, 2)):
             for k in range(2):
-                ref[block, pl.ds(pad - 2 + k, 1), :] = pack_in[0, c, at + k, here, :]
-                ref[block, pl.ds(pad + lanes + k, 1), :] = pack_in[1, c, at + k, here, :]
-        tu_t[block, pl.ds(pad - 1, 1), :] = pack_in[0, c, 4, here, :]
-        tu_t[block, pl.ds(pad + lanes, 1), :] = pack_in[1, c, 4, here, :]
-        ts_t[block, pl.ds(pad - 1, 1), :] = pack_in[0, c, 5, here, :]
+                ref[block, pl.ds(pad - 2 + k, 1), :] = pack_in[c, at + k, here, :]
+                ref[block, pl.ds(pad + lanes + k, 1), :] = pack_in[c, 5 + at + k, here, :]
+        tu_t[block, pl.ds(pad - 1, 1), :] = pack_in[c, 4, here, :]
+        tu_t[block, pl.ds(pad + lanes, 1), :] = pack_in[c, 9, here, :]
 
         def read(ref, i):
             return ref[block, pl.ds(pad + i, group), :]
@@ -371,7 +389,9 @@
             return (read(tu_t, i - 1) + read(tu_t, i)) * q(*[read(um_t, i + k) for k in (-2, -1, 0, 1)])
 
         def east(i):
-            return read(ts_t, i) * q(*[read(vm_t, i + k) for k in (-1, 0, 1, 2)])
+            tu = read(tu_t, i)
+            both = tu + jnp.where(lane % rows == rows - 1, 0.0, roll(tu, -1))
+            return both * q(*[read(vm_t, i + k) for k in (-1, 0, 1, 2)])
 
         count = lanes // group
         fs = [west(i * group) for i in range(count)]
@@ -390,8 +410,9 @@
             for b in range(tall):
                 at = pl.ds(b * group, group)
                 k = (s * tall + b) * group
-                u_part[l, at, :] = u_part[l, at, :] + cu_n[l, at, :] * du[k:k + group]
-                v_part[l, at, :] = v_part[l, at, :] + cv_n[l, at, :] * dv[k:k + group]
+                for parts, c_n, d in ((u_parts, cu_n, du), (v_parts, cv_n, dv)):
+                    ref, to = place(parts, b)
+                    ref[l, to, :] = ref[l, to, :] + c_n[l, at, :] * d[k:k + group]
 
     def every(body, c):
         def run(i, carry):
@@ -410,17 +431,10 @@
         for copy in lon_copies(c):
             copy.start()
         send_band(c + 1)
-
-    for copy in side_copies():
-        copy.wait()
-
-    @pl.when(has_down)
-    def _():
-        corner_down().start()
-
-    @pl.when(has_up)
-    def _():
-        corner_up().start()
+    for c in range(chunks):
+        every(inside, c)
+        if c == (chunks - 1) // 2:
+            forward()
 
     for g in range(groups):
         part = pl.ds(g * group, group)
@@ -469,26 +483,32 @@
 
 def finish_kernel(
     nlat, nlon, levels, rows,
-    fold_ref, u_part, v_part, low_own, high_own, keep, side, up_in, down_in, corner_u, corner_v, band,
-    u_out, v_out,
-    high, high_left, u_low, u_high, v_low, v_high, sem,
+    fold_ref, u_mid, v_mid, low_own, high_own, keep, side, up_in, corner_u, corner_v, band,
+    u_low_in, u_high_in, v_low_in, v_high_in, down_in,
+    u_out, v_out, u_low, u_high, v_low, v_high, high,
+    high_left, sem,
 ):
     lat = lax.axis_index("lat")
     lon = lax.axis_index("lon")
     groups = levels // group
     width = nlon * lanes
     lane = lax.broadcasted_iota(jnp.int32, (group, lanes), 1)
+    top = lat == nlat - 1
+    low_rows = pl.ds(0, group)
+    high_rows = pl.ds(rows - group, group)
     middle = pl.ds(group, rows - 2 * group)
-    low = pl.ds(0, group)
-    top = pl.ds(rows - group, group)
-    first = [
-        pltpu.make_async_copy(a.at[:, middle], b.at[:, middle], sem.at[k])
-        for k, (a, b) in enumerate(((u_part, u_out), (v_part, v_out)))
+    copies = [
+        pltpu.make_async_copy(a, b.at[:, at], sem.at[k])
+        for k, (a, b, at) in enumerate((
+            (u_mid, u_out, middle), (v_mid, v_out, middle),
+            (u_low, u_out, low_rows), (u_high, u_out, high_rows),
+            (v_low, v_out, low_rows), (v_high, v_out, high_rows),
+        ))
     ]
-    for copy in first:
+    for copy in copies[:2]:
         copy.start()
 
-    @pl.when(lat == nlat - 1)
+    @pl.when(top)
     def _():
         start = fold_ref[0]
         own = lax.rem(start - lon * lanes - lane + 2 * width, width)
@@ -511,64 +531,51 @@
                 high[k, part, :] = pick(source, part, own)
             high_left[part, :] = pick(5, part, before)
 
-    @pl.when(lat < nlat - 1)
-    def _():
-        for g in range(groups):
-            part = pl.ds(g * group, group)
-            for k in range(6):
-                high[k, part, :] = down_in[k, part, :]
-            high_left[part, :] = roll(corner_u[...], lanes - 68 - 4 * g)
-
-    def copy_tiles(l, carry):
-        for source, a, b in ((u_part, u_low, u_high), (v_part, v_low, v_high)):
-            a[l] = source[l, low, :]
-            b[l] = source[l, top, :]
-        return carry
-
-    lax.fori_loop(0, levels, copy_tiles, 0, unroll=8)
-
-    views = [ref.reshape(levels * group, lanes) for ref in (u_low, u_high, v_low, v_high)]
-
-    def add(view, g, row, value):
+    def add(ref, g, row, value):
+        view = ref.reshape(levels * group, lanes)
         at = pl.ds(g * group * group + row, group, stride=group)
         view[at, :] = view[at, :] + value
 
     for g in range(groups):
         part = pl.ds(g * group, group)
-        um0, um1, vm0, vm1, _, tv0 = [low_own[k, part, :] for k in range(6)]
-        vm30, vm31, tv31 = [high_own[k, part, :] for k in (2, 3, 4)]
-        um_2, um_1, vm_2, vm_1, tv_1 = [up_in[k, part, :] for k in range(5)]
-        um32, um33, vm32, vm33, tu32, tv32 = [high[k, part, :] for k in range(6)]
-        cu0, cu1, cu30, cu31, cv0, cv1, cv30, cv31, tv1, tv30 = [keep[k, part, :] for k in range(10)]
-        v0, v30, v31, q_west, q_east = [side[k, part, :] for k in range(5)]
-
-        face = tv_1 + roll(jnp.where(lane == 0, roll(corner_v[...], -(66 + 4 * g)), tv_1), -1)
+        um0, um1 = low_own[0, part, :], low_own[1, part, :]
+        um_2, um_1, tv_1 = [up_in[k, part, :] for k in (0, 1, 4)]
+        um32, um33 = high[0, part, :], high[1, part, :]
+        cu0, cu1, cu30, cu31 = [keep[k, part, :] for k in range(4)]
+        v0, v30, v31 = [side[k, part, :] for k in range(3)]
+        corner = roll(corner_v[...], -(66 + 4 * g))
+        face = tv_1 + roll(jnp.where(lane == 0, corner, tv_1), -1)
         f_low = face * q(um_2, um_1, um0, um1)
         d0 = v0 * um_1
-        add(views[0], g, 0, -cu0 * (d0 + f_low))
-        add(views[0], g, 1, cu1 * d0)
+        add(u_low, g, 0, -cu0 * (d0 + f_low))
+        add(u_low, g, 1, cu1 * d0)
+        d30 = v30 * um32
+        add(u_high, g, group - 2, -cu30 * d30)
+        add(u_high, g, group - 1, cu31 * (v31 * (7.0 * um32 - um33) + d30))
+    for copy in copies[2:4]:
+        copy.start()
+
+    for g in range(groups):
+        part = pl.ds(g * group, group)
+        vm0, vm1, tv0 = [low_own[k, part, :] for k in (2, 3, 5)]
+        vm30, vm31, tv31 = [high_own[k, part, :] for k in (2, 3, 4)]
+        vm_2, vm_1, tv_1 = [up_in[k, part, :] for k in (2, 3, 4)]
+        vm32, vm33, tu32, tv32 = [high[k, part, :] for k in (2, 3, 4, 5)]
+        cv0, cv1, cv30, cv31, tv1, tv30 = [keep[k, part, :] for k in range(4, 10)]
+        q_west, q_east = side[3, part, :], side[4, part, :]
         w_low = (tv_1 + tv0) * q(vm_2, vm_1, vm0, vm1)
         d0 = (tv0 + tv1) * vm_1
-        add(views[2], g, 0, -cv0 * (d0 + w_low))
-        add(views[2], g, 1, cv1 * d0)
-        d30 = v30 * um32
-        add(views[1], g, group - 2, -cu30 * d30)
-        add(views[1], g, group - 1, cu31 * (v31 * (7.0 * um32 - um33) + d30))
+        add(v_low, g, 0, -cv0 * (d0 + w_low))
+        add(v_low, g, 1, cv1 * d0)
         d30 = (tv30 + tv31) * vm32
         w_high = (tv31 + tv32) * q(vm30, vm31, vm32, vm33)
-        tu_west = roll(jnp.where(lane == lanes - 1, high_left[part, :], tu32), 1)
-        add(views[3], g, group - 2, -cv30 * d30)
-        add(views[3], g, group - 1, cv31 * (w_high + d30 + (tu32 * q_east - tu_west * q_west)))
-
-    last = [
-        pltpu.make_async_copy(a, b.at[:, at], sem.at[2 + k])
-        for k, (a, b, at) in enumerate((
-            (u_low, u_out, low), (u_high, u_out, top), (v_low, v_out, low), (v_high, v_out, top),
-        ))
-    ]
-    for copy in last:
+        corner = jnp.where(top, high_left[part, :], roll(corner_u[...], lanes - 68 - 4 * g))
+        tu_west = roll(jnp.where(lane == lanes - 1, corner, tu32), 1)
+        add(v_high, g, group - 2, -cv30 * d30)
+        add(v_high, g, group - 1, cv31 * (w_high + d30 + (tu32 * q_east - tu_west * q_west)))
+    for copy in copies[4:]:
         copy.start()
-    for copy in first + last:
+    for copy in copies:
         copy.wait()
 
 
@@ -588,14 +595,16 @@
     hbm = pl.BlockSpec(memory_space=pltpu.HBM)
     block = (levels, rows, lanes)
     line = (levels, lanes)
+    strip = (levels, group, lanes)
     shapes = [
-        block, block,
+        strip, (levels, rows - 2 * group, lanes), strip,
+        strip, (levels, rows - 2 * group, lanes), strip,
         (6,) + line, (6,) + line, (10,) + line, (5,) + line, (5,) + line, (6,) + line,
         (group, lanes), (group, lanes), (nlon, 6) + line,
     ]
     tall = (levels * pitch + pad, lanes)
     turned = (blocks, lanes + 2 * pad, lanes)
-    packs = (2, chunks, 6, blocks_in, lanes)
+    packs = (chunks, 11, blocks_in, lanes)
     dma = pltpu.SemaphoreType.DMA
     V = pltpu.VMEM
     fields = pl.pallas_call(
@@ -607,7 +616,7 @@
             V((4,) + block, f32), V((2,) + block, jnp.int32), V((2, rows, lanes), f32),
             V((4, 4) + line, f32), V((2, 4) + line, jnp.int32),
             V(tall, f32), V(tall, f32), V(block, f32), V(block, f32), V(block, f32),
-            V(turned, f32), V(turned, f32), V(turned, f32), V(turned, f32),
+            V(turned, f32), V(turned, f32), V(turned, f32),
             V(packs, f32), V(packs, f32),
             V((group, lanes), f32), V((sides, group, lanes), f32),
             V((chunks, blocks_in, lanes), f32),
@@ -621,21 +630,21 @@
         ),
         name="exchange",
     )(u, v, eu, ev, su, sv, mu, mv)
-    strip = (levels, group, lanes)
+    u_low, u_mid, u_high, v_low, v_mid, v_high = fields[:6]
+    low_own, high_own, keep, side, up_in, down_in, corner_u, corner_v, band = fields[6:]
+    changed = (u_low, u_high, v_low, v_high, down_in)
+    fixed = (u_mid, v_mid, low_own, high_own, keep, side, up_in, corner_u, corner_v, band)
     result = pl.pallas_call(
         functools.partial(finish_kernel, nlat, nlon, levels, rows),
-        out_shape=[jax.ShapeDtypeStruct(block, f32)] * 2,
-        in_specs=[pl.BlockSpec(memory_space=pltpu.SMEM)] + [vmem] * len(shapes),
-        out_specs=[hbm] * 2,
-        scratch_shapes=[
-            V((6,) + line, f32), V(line, f32),
-            V(strip, f32), V(strip, f32), V(strip, f32), V(strip, f32),
-            dma((6,)),
-        ],
+        out_shape=[jax.ShapeDtypeStruct(block, f32)] * 2 + [V(x.shape, f32) for x in changed],
+        in_specs=[pl.BlockSpec(memory_space=pltpu.SMEM)] + [vmem] * (len(fixed) + len(changed)),
+        out_specs=[hbm] * 2 + [vmem] * len(changed),
+        input_output_aliases={1 + len(fixed) + k: 2 + k for k in range(len(changed))},
+        scratch_shapes=[V(line, f32), dma((6,))],
         compiler_params=pltpu.CompilerParams(vmem_limit_bytes=16 * 1024 * 1024),
         name="finish",
-    )(fold, *fields)
-    return tuple(result)
+    )(fold, *fixed, *changed)
+    return tuple(result[:2])
 
 
 def solution(mesh):

time: 12.7 us -> 12.3 us (0.969)
  Pallas kernels: 11.9 us -> 11.5 us
    pallas_call x1, Pallas kernels: 9.93 us -> 9.45 us  [local(): pl.pallas_call(functools.partial(exchange_kernel, nlat, nlon, levels, row...]
where the time goes in v4:
time: 12.3 us; the launch traced here: 12.1 us
  Pallas kernels  11.5 us (93%)
  between operations  0.66 us (5%)
    pallas_call x1, Pallas kernels, local(): pl.pallas_call(functools.partial(exchange_kernel, nlat, nlon, levels, row...  9.45 us
    pallas_call x1, Pallas kernels, local(): pl.pallas_call(functools.partial(finish_kernel, nlat, nlon, levels, rows)...  2.01 us

profile of v4, /device:TPU:0, one launch (start us, length us, event | category | flops | bytes accessed | tf_op | source)
XLA Modules:
  0.0 12.1 jit_solution(9403455807393745106)
XLA Ops:
  0.6 0.0 copy-start
  0.6 9.4 %exchange.1 = (f32[72,8,128]{2,1,0:T(8,128)S(1)}, f32[72,16,128]{2,1,0:T(8,128)S(1)}, f32[72,8,128]{2,1,0:T(8,128)S(1)}, f32[72,8,128]{2,1,0:T(8,128)S(1)}, f32[...) custom-call(f32[72,32,128]{2,1,0:T(8,128)} %u_hbm.1, ...), custom_call_target="tpu_custom_call" | custom-call | tf_op jit(solution)/shard_map/exchange/pallas_call | solution.py:610
  10.1 0.0 copy-done
  10.1 2.0 %finish.1 = (f32[72,32,128]{2,1,0:T(8,128)}, f32[72,32,128]{2,1,0:T(8,128)}, f32[72,8,128]{2,1,0:T(8,128)S(1)}, f32[72,8,128]{2,1,0:T(8,128)S(1)}, f32[72,8,128]...) custom-call(s32[256]{0:T(256)S(1)} %copy-done, ...), custom_call_target="tpu_custom_call", output_to_operand_aliasing={{2}: (11, {}), {3}: (12, {}), {4}: (13, {}), {5}: (14, {}),... | custom-call | tf_op jit(solution)/shard_map/finish/pallas_call | solution.py:637
Async XLA Ops:
  0.6 9.5 %copy-start = (s32[256]{0:T(256)S(1)}, s32[256]{0:T(256)}, u32[]{:S(2)}) copy-start(s32[256]{0:T(256)} %fold_ref.1) | copy-start | bytes 3076

commit v5 on v4

--- a/solution.py
+++ b/solution.py
@@ -52,7 +52,7 @@
     groups = levels // group
     pitch = rows + pad
     step = next(n for n in (3, 2, 1) if blocks_in % n == 0)
-    loads = 3 if chunks % 3 == 0 else chunks
+    loads = chunks
     depth = levels // loads
     lat = lax.axis_index("lat")
     lon = lax.axis_index("lon")
@@ -433,8 +433,7 @@
         send_band(c + 1)
     for c in range(chunks):
         every(inside, c)
-        if c == (chunks - 1) // 2:
-            forward()
+    forward()
 
     for g in range(groups):
         part = pl.ds(g * group, group)
@@ -588,7 +587,7 @@
     blocks = levels // per
     chunks = chunk_count(levels, per)
     blocks_in = blocks // chunks
-    loads = 3 if chunks % 3 == 0 else chunks
+    loads = chunks
     sides = 1 if nlon == 2 else 2
     pitch = rows + pad
     vmem = pl.BlockSpec(memory_space=pltpu.VMEM)

time: 12.3 us -> 12 us (0.976)
  Pallas kernels: 11.5 us -> 11.2 us
    pallas_call x1, Pallas kernels: 9.45 us -> 9.21 us  [local(): pl.pallas_call(functools.partial(exchange_kernel, nlat, nlon, levels, row...]
where the time goes in v5:
time: 12 us; the launch traced here: 11.9 us
  Pallas kernels  11.2 us (93%)
  between operations  0.66 us (6%)
    pallas_call x1, Pallas kernels, local(): pl.pallas_call(functools.partial(exchange_kernel, nlat, nlon, levels, row...  9.21 us
    pallas_call x1, Pallas kernels, local(): pl.pallas_call(functools.partial(finish_kernel, nlat, nlon, levels, rows)...  2.01 us

profile of v5, /device:TPU:0, one launch (start us, length us, event | category | flops | bytes accessed | tf_op | source)
XLA Modules:
  0.0 11.9 jit_solution(12161838035626559943)
XLA Ops:
  0.6 0.0 copy-start
  0.6 9.2 %exchange.1 = (f32[72,8,128]{2,1,0:T(8,128)S(1)}, f32[72,16,128]{2,1,0:T(8,128)S(1)}, f32[72,8,128]{2,1,0:T(8,128)S(1)}, f32[72,8,128]{2,1,0:T(8,128)S(1)}, f32[...) custom-call(f32[72,32,128]{2,1,0:T(8,128)} %u_hbm.1, ...), custom_call_target="tpu_custom_call" | custom-call | tf_op jit(solution)/shard_map/exchange/pallas_call | solution.py:609
  9.9 0.0 copy-done
  9.9 2.0 %finish.1 = (f32[72,32,128]{2,1,0:T(8,128)}, f32[72,32,128]{2,1,0:T(8,128)}, f32[72,8,128]{2,1,0:T(8,128)S(1)}, f32[72,8,128]{2,1,0:T(8,128)S(1)}, f32[72,8,128]...) custom-call(s32[256]{0:T(256)S(1)} %copy-done, ...), custom_call_target="tpu_custom_call", output_to_operand_aliasing={{2}: (11, {}), {3}: (12, {}), {4}: (13, {}), {5}: (14, {}),... | custom-call | tf_op jit(solution)/shard_map/finish/pallas_call | solution.py:636
Async XLA Ops:
  0.6 9.2 %copy-start = (s32[256]{0:T(256)S(1)}, s32[256]{0:T(256)}, u32[]{:S(2)}) copy-start(s32[256]{0:T(256)} %fold_ref.1) | copy-start | bytes 3076
